TPU v7x, 256 devices: a whole 4x4x8 slice. The times are simulated.
256 devices in a mesh: path: 64 (over z, y, core), dim: 4 (over x).
Axes of the slice: x: 4, y: 4, z: 8, core: 2. Of those that a mesh axis runs over, the one named last changes fastest.
Arguments:
- inner_noise: bfloat16 [512, 1000, 512], P('path', 'dim'), may hold values from -6 to 6
- outer_noise: bfloat16 [1000, 512], P('dim'), may hold values from -6 to 6
- start: float32 [1000], P('dim'), may hold values from 0.8 to 1.25
- vol: float32 [1000], P('dim'), may hold values from 0.1 to 0.4
- times: float32 [512], replicated, may hold values from 0.1 to 0.9
Outputs:
- root_value: float32 [1], replicated
- root_grad: float32 [1000], P('dim')
- point_value: float32 [512], P('path')
- point_grad: float32 [1000, 512], P('dim', 'path')
All inputs are finite; a program needn't handle non-finite values.
Results may differ from a plain program's by a relative error of at most 0.0003.
Values sent between devices are 32-bit elements; how exact they have to be, the bound alone decides.
A program may use at most 64 MiB of HBM per device.

v0:
```python
import jax
import jax.numpy as jnp
from jax import lax
from jax.sharding import PartitionSpec as P

drift = 0.02
delta = 2.0 / 3.0
rate_free = 0.02
gamma_high = 0.2
gamma_low = 0.02
value_high = 0.4
value_low = 0.7


def copy_for_each(array, axis):
    peers = lax.axis_size(axis)
    return lax.all_to_all(
        jnp.broadcast_to(array[None], (peers, *array.shape)), axis, 0, 0, tiled=True
    )


def of_everyone(array, axis):
    return copy_for_each(array, axis).min(axis=0)


def cut_along(array, dim, peers):
    lengths = array.shape
    tiles = array.reshape(*lengths[:dim], peers, lengths[dim] // peers, *lengths[dim + 1 :])
    return jnp.moveaxis(tiles, dim, 0)


def sum_at_owner(array, axis, dim):
    peers = lax.axis_size(axis)
    tiles = lax.all_to_all(cut_along(array, dim, peers), axis, 0, 0, tiled=True)
    return jnp.sum(tiles, axis=0)


def taken_together(array, axis):
    everything = copy_for_each(array, axis)
    return jnp.sum(everything, axis=0)


def in_one(arrays, axis):
    ends = [0]
    for a in arrays:
        ends.append(ends[-1] + a.size)
    subtotal = taken_together(jnp.concatenate([a.ravel() for a in arrays]), axis)
    return tuple((subtotal[b:e].reshape(a.shape) for a, b, e in zip(arrays, ends, ends[1:])))


def driver_of(value):
    slope = jnp.clip((value - value_high) / (value_low - value_high), 0.0, 1.0)
    quota = gamma_high + (gamma_low - gamma_high) * slope
    return -(1.0 - delta) * quota * value - rate_free * value


def per_device(inner_noise, outer_noise, start, vol, times):
    paths_here = inner_noise.shape[0]
    points = times.shape[0]
    groups = lax.axis_size("path")
    inner_total = paths_here * groups
    owned = points // groups
    tau = 1.0 - times
    outer = outer_noise.astype(jnp.float32)
    mean_rate = (drift - 0.5 * vol * vol)[:, None]
    outer_state = start[:, None] * jnp.exp(
        mean_rate * times[None, :] + vol[:, None] * jnp.sqrt(times)[None, :] * outer
    )
    shock = inner_noise.astype(jnp.float32)
    level = outer_state[None] * jnp.exp(
        (mean_rate * tau[None, :])[None] + (vol[:, None] * jnp.sqrt(tau)[None, :])[None] * shock
    )
    local_min = jnp.min(level, axis=1)
    payoff = of_everyone(local_min, "dim")
    totals = jnp.sum(payoff, axis=0)
    moments = jnp.sum(payoff[:, None, :] * shock, axis=0)
    start_index = lax.axis_index("path") * owned
    own_totals, own_moments = (sum_at_owner(totals, "path", 0), sum_at_owner(moments, "path", 1))
    own_times = lax.dynamic_slice_in_dim(times, start_index, owned, 0)
    own_tau = 1.0 - own_times
    own_state = lax.dynamic_slice_in_dim(outer_state, start_index, owned, 1)
    own_outer = lax.dynamic_slice_in_dim(outer, start_index, owned, 1)
    own_value = own_totals / inner_total
    own_grad = own_moments / (inner_total * vol[:, None] * own_state * jnp.sqrt(own_tau)[None, :])
    driver = driver_of(own_value)
    terminal = jnp.sum(
        jnp.sqrt(own_times)[None, :] * own_outer * own_totals[None, :]
        + jnp.sqrt(own_tau)[None, :] * own_moments,
        axis=1,
    )
    integral = jnp.sum(driver[None, :] * own_outer / jnp.sqrt(own_times)[None, :], axis=1)
    payoff_sum, driver_sum, terminal, integral = in_one(
        (jnp.sum(own_totals), jnp.sum(driver), terminal, integral), "path"
    )
    root_value = payoff_sum / (points * inner_total) + driver_sum / points
    root_grad = terminal / (points * inner_total * vol * start) + integral / (points * vol * start)
    return (jnp.reshape(root_value, (1,)), root_grad, own_value, own_grad)


def solution(mesh):
    in_specs = (P("path", "dim", None), P("dim", None), P("dim"), P("dim"), P())
    out_specs = (P(), P("dim"), P("path"), P("dim", "path"))
    return jax.shard_map(
        per_device, mesh=mesh, in_specs=in_specs, out_specs=out_specs, check_vma=False
    )
```

profile of v0, /device:TPU:1, one launch (start us, length us, event | category | flops | bytes accessed | tf_op | source)
XLA Modules:
  0.0 89.9 jit_solution(10215479354179865058)
XLA Ops:
  0.6 0.7 fusion.11
  1.3 0.7 broadcast_multiply_fusion.2
  2.0 1.1 %copy.29 = bf16[250,512]{0,1:T(8,128)(2,1)S(1)} copy(bf16[250,512]{1,0:T(8,128)(2,1)} %param.6) | data formatting | bytes 512000 | tf_op args[1]
  3.1 0.0 copy-start
  3.1 2.2 %exponential_multiply_fusion = (f32[250,512]{0,1:T(8,128)S(1)}, f32[250,512]{0,1:T(8,128)}, f32[250,512]{0,1:T(8,128)}) fusion(f32[512]{0:T(512)S(1)} %get-tuple-element.16, f32[250]{0:T(256)} %param.8, f32[512]{0:T(512)} %param.9, f32[250]{0:T(256)S(1)} %get-tuple-element.20, f32[250]{0:T(256)} %param.7, bf16[250,512]{0,1:T(8,128)(2,1)S(1)} %copy.29, ...), kind=kLoop, calls=%fused_computation.7 | loop fusion | flops 1024000 | bytes 1803192 | tf_op jit(solution)/shard_map/mul | solution.py:66
  5.3 1.2 %copy.32 = f32[250,512]{1,0:T(8,128)S(1)} copy(f32[250,512]{0,1:T(8,128)} %get-tuple-element.23) | data formatting | bytes 1024000 | tf_op jit(solution)/shard_map/mul | solution.py:71
  6.5 2.1 %copy.31 = f32[250,512]{1,0:T(8,128)} copy(f32[250,512]{0,1:T(8,128)} %get-tuple-element.22) | data formatting | bytes 1024000 | tf_op jit(solution)/shard_map/mul | solution.py:71
  8.6 1.0 %copy.30 = f32[250,512]{1,0:T(8,128)} copy(f32[250,512]{0,1:T(8,128)S(1)} %get-tuple-element.21) | data formatting | bytes 1024000 | tf_op jit(solution)/shard_map/mul | solution.py:66
  9.6 0.0 copy-done
  9.6 2.1 %fusion.3 = f32[8,512]{1,0:T(8,128)S(1)} fusion(bf16[8,250,512]{2,0,1:T(8,128)(2,1)S(1)} %copy-done, f32[250,512]{1,0:T(8,128)S(1)} %copy.32, f32[250,512]{1,0:T(8,128)} %copy.31, f32[250,512]{1,0:T(8,128)} %copy.30), kind=kLoop, calls=%fused_computation.5 | loop fusion | flops 5115904 | bytes 3600384 | tf_op jit(solution)/shard_map/reduce_min | solution.py:73
  11.7 9.1 %all_to_all.25 = f32[4,8,512]{2,1,0:T(8,128)S(1)} all-to-all(f32[4,8,512]{2,1,0:T(8,128)S(1)} %broadcast_in_dim.4), channel_id=1, replica_groups=mesh['path'=64,'dim'=4] {'dim'}, dimensions={0} | all-to-all | bytes 131072 | tf_op jit(solution)/shard_map/all_to_all | solution.py:17
  20.8 0.7 all_to_all.17
  21.5 13.8 %all-to-all-start.1 = ((f32[64,1,8]{2,1,0:T(1,128)}), f32[64,1,8]{2,1,0:T(1,128)S(1)}, u32[]{:S(2)}, u32[]{:S(2)}) async-start(f32[64,1,8]{2,1,0:T(1,128)} %bitcast), calls=%async_computation.1 | async-start | bytes 65536 | tf_op jit(solution)/shard_map/all_to_all | solution.py:34
  35.3 1.4 %fusion.4 = f32[250,512]{1,0:T(8,128)S(1)} fusion(bf16[8,250,512]{2,0,1:T(8,128)(2,1)S(1)} %copy-done, f32[8,512]{1,0:T(8,128)S(1)} %reduce_min.19), kind=kLoop, calls=%fused_computation.6 | loop fusion | flops 2944000 | bytes 2576384 | tf_op jit(solution)/shard_map/reduce_sum | solution.py:76
  36.7 0.0 copy-start.1
  36.7 0.0 copy-start.2
  36.7 1.0 %copy.34 = f32[250,512]{0,1:T(8,128)} copy(f32[250,512]{1,0:T(8,128)S(1)} %fusion.4) | data formatting | bytes 1024000 | tf_op jit(solution)/shard_map/reduce_sum | solution.py:76
  37.7 7.0 %all-to-all-done.1 = f32[64,1,8]{2,1,0:T(1,128)S(1)} async-done(((f32[64,1,8]{2,1,0:T(1,128)}), f32[64,1,8]{2,1,0:T(1,128)S(1)}, u32[]{:S(2)}, u32[]{:S(2)}) %all-to-all-start.1) | async-done | bytes 2080 | tf_op jit(solution)/shard_map/all_to_all | solution.py:34
  44.7 4.7 %all-to-all-start.2 = ((f32[64,250,8]{1,2,0:T(8,128)}), f32[64,250,8]{1,2,0:T(8,128)S(1)}, u32[]{:S(2)}, u32[]{:S(2)}) async-start(f32[64,250,8]{1,2,0:T(8,128)} %bitcast.4), calls=%async_computation.2 | async-start | bytes 1048576 | tf_op jit(solution)/shard_map/all_to_all | solution.py:34
  49.5 0.8 dynamic-slice_sqrt_fusion
  50.2 0.7 fusion.8
  50.9 1.1 %fusion.9 = (f32[]{:T(128)}, f32[8]{0:T(128)S(1)}, f32[8]{0:T(128)}) fusion(f32[8]{0:T(128)S(1)} %get-tuple-element.7), kind=kLoop, calls=%fused_computation.26 | loop fusion | flops 87 | bytes 100 | tf_op jit(solution)/shard_map/reduce_sum | solution.py:93
  52.0 15.2 %all-to-all-done.2 = f32[64,250,8]{1,2,0:T(8,128)S(1)} async-done(((f32[64,250,8]{1,2,0:T(8,128)}), f32[64,250,8]{1,2,0:T(8,128)S(1)}, u32[]{:S(2)}, u32[]{:S(2)}) %all-to-all-start.2) | async-done | bytes 512032 | tf_op jit(solution)/shard_map/all_to_all | solution.py:34
  67.2 0.1 reduce_sum.86
  67.3 0.7 add_reduce_fusion
  68.0 1.4 %pad_maximum_fusion = f32[502]{0:T(512)S(1)} fusion(f32[250]{0:T(256)S(1)} %get-tuple-element.5, f32[250]{0:T(256)S(1)} %get-tuple-element.4, f32[1]{0:T(128)} %bitcast.2, f32[1]{0:T(128)} %bitcast.1), kind=kLoop, calls=%fused_computation.14 | loop fusion | flops 1506 | bytes 4016 | tf_op jit(solution)/shard_map/concatenate | solution.py:47
  69.4 0.1 broadcast_in_dim.5
  69.4 16.6 %all_to_all.26 = f32[64,1,502]{2,1,0:T(1,128)S(1)} all-to-all(f32[64,1,502]{2,1,0:T(1,128)S(1)} %broadcast_in_dim.5), channel_id=1, replica_groups=mesh['path'=64,'dim'=4] {'path'}, dimensions={0} | all-to-all | bytes 257024 | tf_op jit(solution)/shard_map/all_to_all | solution.py:17
  86.0 0.1 reduce_sum.89
  86.1 0.6 fusion.10
  86.7 0.0 copy-done.1
  86.7 0.0 copy-done.2
  86.7 0.6 divide_add_fusion
  (4 shorter events, 0.1 us)
Async XLA Ops:
  3.1 6.5 %copy-start = (bf16[8,250,512]{2,0,1:T(8,128)(2,1)S(1)}, bf16[8,250,512]{2,0,1:T(8,128)(2,1)}, u32[]{:S(2)}) copy-start(bf16[8,250,512]{2,0,1:T(8,128)(2,1)} %param.5) | copy-start | bytes 6144004
  21.5 23.2 %all-to-all-start.1 = ((f32[64,1,8]{2,1,0:T(1,128)}), f32[64,1,8]{2,1,0:T(1,128)S(1)}, u32[]{:S(2)}, u32[]{:S(2)}) async-start(f32[64,1,8]{2,1,0:T(1,128)} %bitcast), calls=%async_computation.1 | async-start | bytes 65536 | tf_op jit(solution)/shard_map/all_to_all | solution.py:34
  36.7 50.1 %copy-start.1 = (f32[250]{0:T(256)S(1)}, f32[250]{0:T(256)}, u32[]{:S(2)}) copy-start(f32[250]{0:T(256)} %param.8) | copy-start | bytes 3004
  36.7 50.1 %copy-start.2 = (f32[250]{0:T(256)S(1)}, f32[250]{0:T(256)}, u32[]{:S(2)}) copy-start(f32[250]{0:T(256)} %param.7) | copy-start | bytes 3004
  44.7 22.5 %all-to-all-start.2 = ((f32[64,250,8]{1,2,0:T(8,128)}), f32[64,250,8]{1,2,0:T(8,128)S(1)}, u32[]{:S(2)}, u32[]{:S(2)}) async-start(f32[64,250,8]{1,2,0:T(8,128)} %bitcast.4), calls=%async_computation.2 | async-start | bytes 1048576 | tf_op jit(solution)/shard_map/all_to_all | solution.py:34
where the time goes:
time: 90.4 us; the launch traced here: 89.9 us
  blocking collectives  25.7 us (28%)
  waiting for transfers between devices  22.2 us (25%)
  starting transfers between devices  18.5 us (20%)
  other arithmetic  12.5 us (14%)
  local copies, waits for them, and re-layouts  7.74 us (9%)
  between operations  3.21 us (4%)
    all_to_all x2, blocking collectives, copy_for_each(): lax.all_to_all(jnp.broadcast_to(array[None], (peers, *array.shape)), axis...  25.7 us
    all_to_all x2, waiting for transfers between devices, sum_at_owner(): tiles = lax.all_to_all(cut_along(array, dim, peers), axis, 0, 0, tiled=True)  22.2 us
    all_to_all x2, starting transfers between devices, sum_at_owner(): tiles = lax.all_to_all(cut_along(array, dim, peers), axis, 0, 0, tiled=True)  18.5 us
    mul x1, other arithmetic, per_device(): start[:, None]  2.19 us
    reduce_min x1, other arithmetic, per_device(): local_min = jnp.min(level, axis=1)  2.09 us
    mul x1, local copies, waits for them, and re-layouts, per_device(): mean_rate * tau[None, :]  2.05 us
  transfers between devices with their start and end apart: 2, of which 2 were waited for; matrix products, arithmetic and copies ran while one was open for 5% of the time, Pallas kernels for 0%

commit v1 on v0

v1 whole, which is shorter than its diff:
```python
import functools

import jax
import jax.numpy as jnp
from jax import lax
from jax.experimental import pallas as pl
from jax.experimental.pallas import tpu as pltpu
from jax.sharding import PartitionSpec as P

drift = 0.02
delta = 2.0 / 3.0
rate_free = 0.02
gamma_high = 0.2
gamma_low = 0.02
value_high = 0.4
value_low = 0.7

NX, NY, NZ, NC = 4, 4, 8, 2
MESH = pl.DeviceIdType.MESH
F32 = jnp.float32
BF16 = jnp.bfloat16
CHUNKS = 5
PAIRS = (2, 1, 3, 0)


def driver_of(value):
    slope = jnp.clip((value - value_high) / (value_low - value_high), 0.0, 1.0)
    quota = gamma_high + (gamma_low - gamma_high) * slope
    return -(1.0 - delta) * quota * value - rate_free * value


def kernel(
    noise_hbm, outer_hbm, start_hbm, vol_hbm, times_hbm,
    rv_ref, rg_ref, pv_ref, pg_ref,
    noise, outer, start_v, vol_v, times_v,
    startp, volp, volb, abase, lmin, rx, pay, stage, nt, rc, ry, rz, scm, smy, smz, tot, dinv,
    in_sem, sx_s, sx_r, sc_s, sc_r, sy_s, sy_r, sz_s, sz_r, smc_s, smc_r, smy_s, smy_r, smz_s, smz_r,
):
    D, K, M = noise.shape
    path = lax.axis_index("path")
    x = lax.axis_index("dim")
    z = path // (NY * NC)
    y = (path // NC) % NY
    c = path % NC
    jz = z // 2

    def at_x(k):
        return (path, (x + k) % NX)

    def at(zz, yy, cc):
        return ((zz * NY + yy) * NC + cc, x)

    barrier = pltpu.get_barrier_semaphore()
    for k in range(1, NZ):
        pl.semaphore_signal(barrier, inc=1, device_id=at((z + k) % NZ, y, c), device_id_type=MESH)
    for k in range(1, NY):
        pl.semaphore_signal(barrier, inc=1, device_id=at(z, (y + k) % NY, c), device_id_type=MESH)
    for k in range(1, NX):
        pl.semaphore_signal(barrier, inc=1, device_id=at_x(k), device_id_type=MESH)
    pl.semaphore_signal(barrier, inc=1, device_id=at(z, y, 1 - c), device_id_type=MESH)

    small_in = [
        pltpu.make_async_copy(vol_hbm, vol_v, in_sem.at[0]),
        pltpu.make_async_copy(start_hbm, start_v, in_sem.at[1]),
        pltpu.make_async_copy(times_hbm, times_v, in_sem.at[2]),
        pltpu.make_async_copy(outer_hbm, outer, in_sem.at[3]),
    ]
    for cp in small_in:
        cp.start()
    per = D // CHUNKS
    noise_in = [
        pltpu.make_async_copy(
            noise_hbm.at[pl.ds(q * per, per)], noise.at[pl.ds(q * per, per)], in_sem.at[4 + q]
        )
        for q in range(CHUNKS)
    ]
    for cp in noise_in:
        cp.start()
    for cp in small_in:
        cp.wait()

    startp[...] = jnp.ones_like(startp)
    volp[...] = jnp.ones_like(volp)
    startp[:, 0:D] = start_v[...]
    volp[:, 0:D] = vol_v[...]
    vol = volp[...]
    begin = startp[...]
    times = times_v[...]
    tau = 1.0 - times
    root_t = jnp.sqrt(times)
    root_tau = jnp.sqrt(tau)
    inv_root_tau = 1.0 / root_tau
    offset = jnp.log(begin) + (drift - 0.5 * vol * vol)
    for h in range(2):
        volb[h * 128 : (h + 1) * 128, :] = jnp.broadcast_to(
            vol[:, h * 128 : (h + 1) * 128], (128, 128)
        ).T
        stage[h * 128 : (h + 1) * 128, :] = jnp.broadcast_to(
            offset[:, h * 128 : (h + 1) * 128], (128, 128)
        ).T
    for lo in range(0, D, 16):
        hi = min(lo + 16, D)
        for j in range(4):
            ls = slice(j * 128, (j + 1) * 128)
            o = outer[lo:hi, ls].astype(F32)
            abase[j, lo:hi, :] = (
                stage[lo:hi, :] + volb[lo:hi, :] * (root_t[:, ls] * o)
            ) * inv_root_tau[:, ls]

    acc = tuple(jnp.full((K, 128), 3.0e38, F32) for _ in range(4))
    unroll = 10
    for q in range(CHUNKS):
        noise_in[q].wait()

        def body(g, acc, q=q):
            acc = list(acc)
            for u in range(unroll):
                d = q * per + g * unroll + u
                v = volb[pl.ds(d, K, stride=0), :]
                for j in range(4):
                    n = noise[d, :, j * 128 : (j + 1) * 128].astype(F32)
                    a = abase[j, pl.ds(d, K, stride=0), :]
                    acc[j] = jnp.minimum(acc[j], n * v + a)
            return tuple(acc)

        acc = lax.fori_loop(0, per // unroll, body, acc)
    for j in range(4):
        lmin[:, j * 128 : (j + 1) * 128] = acc[j]

    pl.semaphore_wait(barrier, (NZ - 1) + (NY - 1) + (NX - 1) + 1)

    x_copies = []
    for k in (2, 1, 3):
        cp = pltpu.make_async_remote_copy(
            src_ref=lmin, dst_ref=rx.at[k - 1], send_sem=sx_s.at[k - 1], recv_sem=sx_r.at[k - 1],
            device_id=at_x(k), device_id_type=MESH,
        )
        cp.start()
        x_copies.append(cp)

    lane = lax.broadcasted_iota(jnp.int32, (K, M), 1)
    row = lax.broadcasted_iota(jnp.int32, (K, M), 0)
    pick = lane == path * K + row
    own_t = jnp.sum(jnp.where(pick, times, 0.0), axis=1, keepdims=True)
    own_outer = lax.dot_general(
        jnp.where(pick, 1.0, 0.0).astype(BF16), outer[...], (((1,), (1,)), ((), ())),
        preferred_element_type=F32,
    )
    vol_d = vol_v[...]
    own_state = start_v[...] * jnp.exp(
        (drift - 0.5 * vol_d * vol_d) * own_t + vol_d * jnp.sqrt(own_t) * own_outer
    )
    dinv[...] = 1.0 / ((K * NZ * NY * NC) * vol_d * own_state * (1.0 - own_t))

    for cp in x_copies:
        cp.wait_recv()
    least = jnp.minimum(jnp.minimum(lmin[...], rx[0]), jnp.minimum(rx[1], rx[2]))
    payoff = jnp.exp(root_tau * least)
    pay[...] = payoff * root_tau
    totals = jnp.sum(payoff, axis=0, keepdims=True)

    sub = lax.broadcasted_iota(jnp.int32, (8, 128), 0)
    bit2 = (sub & 4) == 0
    bit1 = (sub & 2) == 0
    bit0 = (sub & 1) == 0

    def merge(a, b, first, shift):
        if shift == 4:
            return jnp.where(first, a, b) + pltpu.roll(jnp.where(first, b, a), 4, axis=0)
        return jnp.where(
            first,
            a + pltpu.roll(a, 8 - shift, axis=0),
            b + pltpu.roll(b, shift, axis=0),
        )

    def sums_of(ys):
        c4 = [merge(ys[s], ys[s + 4], bit2, 4) for s in range(4)]
        e2 = [merge(c4[s], c4[s + 2], bit1, 2) for s in range(2)]
        return merge(e2[0], e2[1], bit0, 1)

    def core_copy(t):
        return pltpu.make_async_remote_copy(
            src_ref=nt.at[t, 1 - c], dst_ref=rc.at[t], send_sem=sc_s.at[t], recv_sem=sc_r.at[t],
            device_id=at(z, y, 1 - c), device_id_type=MESH,
        )

    def y_copy(t, k):
        peer = (y + k) % NY
        return pltpu.make_async_remote_copy(
            src_ref=nt.at[t, c, peer], dst_ref=ry.at[t, k - 1],
            send_sem=sy_s.at[t * 3 + k - 1], recv_sem=sy_r.at[t * 3 + k - 1],
            device_id=at(z, peer, c), device_id_type=MESH,
        )

    def after_core(t):
        core_copy(t).wait_recv()
        nt[t, c] = nt[t, c] + rc[t]
        for k in (2, 1, 3):
            y_copy(t, k).start()

    wsum = jnp.zeros((8, 256), F32)
    full = D // 8
    for t, off in enumerate(PAIRS):
        j = (jz + off) % 4
        lanes = pl.ds(pl.multiple_of(j * 128, 128), 128)
        p = pay[:, lanes]

        def group(g, _, p=p, lanes=lanes):
            ys = [noise[g * 8 + s, :, lanes].astype(F32) * p for s in range(8)]
            stage[pl.ds(pl.multiple_of(g * 8, 8), 8), :] = sums_of(ys)
            return 0

        lax.fori_loop(0, full, group, 0)
        rest = [noise[full * 8 + s, :, lanes].astype(F32) * p for s in range(D - full * 8)]
        rest += [jnp.zeros((8, 128), F32)] * (8 - len(rest))
        stage[full * 8 : full * 8 + 8, :] = sums_of(rest)
        for h in range(2):
            block = stage[h * 128 : (h + 1) * 128, :].T
            part = jnp.zeros((8, 128), F32)
            for q in range(16):
                zz, yy, cc = q // 8, (q // 2) % 4, q % 2
                piece = block[q * 8 : (q + 1) * 8, :]
                nt[t, cc, yy, zz, :, h * 128 : (h + 1) * 128] = piece
                part = part + piece
            wsum = wsum + (
                jnp.concatenate([part, jnp.zeros((8, 128), F32)], axis=1)
                if h == 0
                else jnp.concatenate([jnp.zeros((8, 128), F32), part], axis=1)
            )
        if t == 3:
            w = jnp.sum(wsum, axis=0, keepdims=True)
            scm[0] = jnp.concatenate(
                [totals[:, k * 128 : (k + 1) * 128] for k in range(4)]
                + [w[:, 0:128], w[:, 128:256], jnp.zeros((2, 128), F32)],
                axis=0,
            )
            small_core = pltpu.make_async_remote_copy(
                src_ref=scm.at[0], dst_ref=scm.at[1], send_sem=smc_s, recv_sem=smc_r,
                device_id=at(z, y, 1 - c), device_id_type=MESH,
            )
            small_core.start()
        core_copy(t).start()
        if t >= 1:
            after_core(t - 1)

    small_core.wait_recv()
    smy[y] = scm[0] + scm[1]
    small_y = []
    for k in (2, 1, 3):
        cp = pltpu.make_async_remote_copy(
            src_ref=smy.at[y], dst_ref=smy.at[y], send_sem=smy_s.at[k - 1], recv_sem=smy_r.at[k - 1],
            device_id=at(z, (y + k) % NY, c), device_id_type=MESH,
        )
        cp.start()
        small_y.append(cp)
    after_core(3)

    def z_copy(t, peer, zz):
        return pltpu.make_async_remote_copy(
            src_ref=nt.at[t, c, y, zz], dst_ref=rz.at[z], send_sem=sz_s.at[peer], recv_sem=sz_r.at[z],
            device_id=at(peer, y, c), device_id_type=MESH,
        )

    def after_y(t):
        for k in range(1, NY):
            y_copy(t, k).wait_recv()
        nt[t, c, y] = nt[t, c, y] + (ry[t, 0] + ry[t, 1] + ry[t, 2])
        base = 2 * ((jz + PAIRS[t]) % 4)
        if PAIRS[t] == 0:
            peer = base + 1 - z % 2
            z_copy(t, peer, 1 - z % 2).start()
        else:
            for zz in range(2):
                z_copy(t, base + zz, zz).start()

    after_y(0)
    for cp in small_y:
        cp.wait_recv()
    smz[z] = (smy[0] + smy[1]) + (smy[2] + smy[3])
    small_z = []
    for k in (4, 3, 5, 2, 6, 1, 7):
        cp = pltpu.make_async_remote_copy(
            src_ref=smz.at[z], dst_ref=smz.at[z], send_sem=smz_s.at[k - 1], recv_sem=smz_r.at[k - 1],
            device_id=at((z + k) % NZ, y, c), device_id_type=MESH,
        )
        cp.start()
        small_z.append(cp)
    after_y(1)
    after_y(2)
    after_y(3)

    for cp in small_z:
        cp.wait_recv()
    whole = ((smz[0] + smz[1]) + (smz[2] + smz[3])) + ((smz[4] + smz[5]) + (smz[6] + smz[7]))
    inner = K * NZ * NY * NC
    tot[...] = whole
    totals = jnp.concatenate([whole[k : k + 1, :] for k in range(4)], axis=1)
    driver = driver_of(totals * (1.0 / inner))
    rv_ref[...] = (
        jnp.sum(totals, axis=1, keepdims=True) * (1.0 / (M * inner))
        + jnp.sum(driver, axis=1, keepdims=True) * (1.0 / M)
    )
    weight = root_t * totals * (1.0 / (M * inner)) + driver / (root_t * M)
    w_hi = weight.astype(BF16).astype(F32)
    w_mid = (weight - w_hi).astype(BF16).astype(F32)
    w_lo = weight - w_hi - w_mid
    rows = lax.broadcasted_iota(jnp.int32, (8, M), 0)
    lhs = jnp.where(rows == 0, w_hi, jnp.where(rows == 1, w_mid, jnp.where(rows == 2, w_lo, 0.0)))
    prod = lax.dot_general(
        lhs.astype(BF16), outer[...], (((1,), (1,)), ((), ())), preferred_element_type=F32
    )
    noise_sum = jnp.sum(prod, axis=0, keepdims=True)
    moment_sum = jnp.concatenate([whole[4:5, :], whole[5:6, :]], axis=1)[:, 0:D]
    rg_ref[...] = (noise_sum + moment_sum * (1.0 / (M * inner))) / (vol_v[...] * start_v[...])
    own_row = tot[pl.ds(path // 16, 1), :] * (1.0 / inner)
    own_row = pltpu.roll(jnp.broadcast_to(own_row, (8, 128)), (128 - (path % 16) * 8) % 128, axis=1)
    pv_ref[...] = own_row[0:1, 0:8]

    own = nt[3, c, y, z % 2]
    for k in range(1, NZ):
        src = (z + k) % NZ
        pltpu.make_async_remote_copy(
            src_ref=rz.at[src], dst_ref=rz.at[src], send_sem=sz_s.at[src], recv_sem=sz_r.at[src],
            device_id=at(src, y, c), device_id_type=MESH,
        ).wait_recv()
        own = own + rz[src]
    pg_ref[...] = own[:, 0:D] * dinv[...]

    for cp in x_copies + small_y + small_z + [small_core]:
        cp.wait_send()
    for t in range(4):
        core_copy(t).wait_send()
        for k in range(1, NY):
            y_copy(t, k).wait_send()
    for k in range(1, NZ):
        peer = (z + k) % NZ
        pltpu.make_async_remote_copy(
            src_ref=rz.at[peer], dst_ref=rz.at[peer], send_sem=sz_s.at[peer], recv_sem=sz_r.at[peer],
            device_id=at(peer, y, c), device_id_type=MESH,
        ).wait_send()


def per_device(inner_noise, outer_noise, start, vol, times):
    K, D, M = inner_noise.shape
    hbm = pl.BlockSpec(memory_space=pltpu.HBM)
    vmem = pl.BlockSpec(memory_space=pltpu.VMEM)
    dma = pltpu.SemaphoreType.DMA
    V = pltpu.VMEM
    root_value, root_grad, point_value, point_grad = pl.pallas_call(
        kernel,
        out_shape=(
            jax.ShapeDtypeStruct((1, 1), F32),
            jax.ShapeDtypeStruct((1, D), F32),
            jax.ShapeDtypeStruct((1, 8), F32),
            jax.ShapeDtypeStruct((8, D), F32),
        ),
        in_specs=[hbm] * 5,
        out_specs=(vmem,) * 4,
        scratch_shapes=[
            V((D, K, M), BF16), V((D, M), BF16), V((1, D), F32), V((1, D), F32), V((1, M), F32),
            V((1, 256), F32), V((1, 256), F32), V((256, 128), F32), V((4, 256, 128), F32),
            V((K, M), F32), V((3, K, M), F32), V((K, M), F32), V((256, 128), F32),
            V((4, NC, NY, 2, 8, 256), F32), V((4, NY, 2, 8, 256), F32),
            V((4, 3, 2, 8, 256), F32), V((NZ, 8, 256), F32),
            V((2, 8, 128), F32), V((NY, 8, 128), F32), V((NZ, 8, 128), F32), V((8, 128), F32),
            V((8, D), F32),
            dma((4 + CHUNKS,)), dma((3,)), dma((3,)), dma((4,)), dma((4,)), dma((12,)), dma((12,)),
            dma((NZ,)), dma((NZ,)), dma, dma, dma((3,)), dma((3,)), dma((7,)), dma((7,)),
        ],
        compiler_params=pltpu.CompilerParams(
            collective_id=0, has_side_effects=True, vmem_limit_bytes=32 * 1024 * 1024
        ),
    )(
        jnp.transpose(inner_noise, (1, 0, 2)), outer_noise, start[None], vol[None], times[None]
    )
    return root_value[0], root_grad[0], point_value[0], point_grad.T


def solution(mesh):
    in_specs = (P("path", "dim", None), P("dim", None), P("dim"), P("dim"), P())
    out_specs = (P(), P("dim"), P("path"), P("dim", "path"))
    return jax.shard_map(
        per_device, mesh=mesh, in_specs=in_specs, out_specs=out_specs, check_vma=False
    )
```

time: 90.4 us -> 33.8 us (0.37)
  blocking collectives: 25.7 us -> 0 us
  Pallas kernels: 0 us -> 25 us
  waiting for transfers between devices: 22.2 us -> 0 us
  starting transfers between devices: 18.5 us -> 0 us
  other arithmetic: 12.5 us -> 0 us
  local copies, waits for them, and re-layouts: 7.74 us -> 6.23 us
    all_to_all x2 -> x0, blocking collectives: 25.7 us -> none  [copy_for_each(): lax.all_to_all(jnp.broadcast_to(array[None], (peers, *array.shape)), axis...]
    pallas_call x0 -> x1, Pallas kernels: none -> 25 us  [per_device(): pl.pallas_call(kernel, out_shape=(jax.ShapeDtypeStruct((1, 1), F32), jax....]
    all_to_all x2 -> x0, waiting for transfers between devices: 22.2 us -> none  [sum_at_owner(): tiles = lax.all_to_all(cut_along(array, dim, peers), axis, 0, 0, tiled=True)]
    all_to_all x2 -> x0, starting transfers between devices: 18.5 us -> none  [sum_at_owner(): tiles = lax.all_to_all(cut_along(array, dim, peers), axis, 0, 0, tiled=True)]
    unnamed x7 -> x13, local copies, waits for them, and re-layouts: 1.1 us -> 6.23 us
    mul x3 -> x0, local copies, waits for them, and re-layouts: 4.28 us -> none  [the longest x1 2.05 us: per_device(): mean_rate * tau[None, :]]
    reduce_sum x7 -> x0, other arithmetic: 4.03 us -> none  [the longest x1 1.35 us: per_device(): moments = jnp.sum(payoff[:, None, :] * shock, axis=0)]
    mul x2 -> x0, other arithmetic: 2.88 us -> none  [the longest x1 2.19 us: per_device(): start[:, None]]
  transfers between devices with their start and end apart: 2 -> 0, of which waited for: 2 -> 0; matrix products, arithmetic and copies ran while one was open for 5% -> 0% of each run, Pallas kernels for 0% -> 0%
where the time goes in v1:
time: 33.8 us; the launch traced here: 33.6 us
  Pallas kernels  25 us (74%)
  local copies, waits for them, and re-layouts  6.23 us (18%)
  between operations  2.34 us (7%)
    pallas_call x1, Pallas kernels, per_device(): pl.pallas_call(kernel, out_shape=(jax.ShapeDtypeStruct((1, 1), F32), jax....  25 us
    unnamed x13, local copies, waits for them, and re-layouts  6.23 us

profile of v1, /device:TPU:1, one launch (start us, length us, event | category | flops | bytes accessed | tf_op | source)
XLA Modules:
  0.0 33.6 jit_solution(15279601740246115376)
XLA Ops:
  0.6 0.0 copy-start
  0.6 1.6 %copy-done = bf16[8,250,512]{2,0,1:T(8,128)(2,1)S(1)} copy-done((bf16[8,250,512]{2,0,1:T(8,128)(2,1)S(1)}, bf16[8,250,512]{2,0,1:T(8,128)(2,1)}, u32[]{:S(2)}) %copy-start) | copy-done | bytes 2048024
  2.2 0.0 copy-start.1
  2.2 0.9 %copy-done.1 = bf16[250,512]{1,0:T(8,128)(2,1)S(1)} copy-done((bf16[250,512]{1,0:T(8,128)(2,1)S(1)}, bf16[250,512]{1,0:T(8,128)(2,1)}, u32[]{:S(2)}) %copy-start.1) | copy-done | bytes 256024
  3.2 0.0 copy-start.2
  3.2 0.7 %copy-done.2 = f32[512]{0:T(512)S(1)} copy-done((f32[512]{0:T(512)S(1)}, f32[512]{0:T(512)}, u32[]{:S(2)}) %copy-start.2) | copy-done | bytes 2072
  3.8 0.0 copy-start.3
  3.8 0.7 %copy-done.3 = f32[250]{0:T(256)S(1)} copy-done((f32[250]{0:T(256)S(1)}, f32[250]{0:T(256)}, u32[]{:S(2)}) %copy-start.3) | copy-done | bytes 1024
  4.5 0.0 copy-start.4
  4.5 0.7 %copy-done.4 = f32[250]{0:T(256)S(1)} copy-done((f32[250]{0:T(256)S(1)}, f32[250]{0:T(256)}, u32[]{:S(2)}) %copy-start.4) | copy-done | bytes 1024
  5.2 25.0 %shard_map.84 = (f32[1,1]{1,0:T(1,128)}, f32[1,250]{1,0:T(1,128)S(1)}, f32[1,8]{1,0:T(1,128)S(1)}, f32[8,250]{1,0:T(8,128)S(1)}) custom-call(bf16[250,8,512]{2,1,0:T(8,128)(2,1)S(1)} %bitcast.8, bf16[250,512]{1,0:T(8,128)(2,1)S(1)} %copy-done.1, f32[1,250]{1,0:T(1,128)S(1)} %bitcast.11, f32[1,250]{1,0:T(1,128)S(1)} %bitcast.12, f32[1,512]{1,0:T(1,128)S(1)} %bitcast.10), custom_call_target="tpu_custom_call" | custom-call | tf_op jit(solution)/shard_map/pallas_call | solution.py:349
  30.8 0.6 %copy.14 = f32[250]{0:T(256)} copy(f32[250]{0:T(256)S(1)} %bitcast.13) | data formatting | bytes 2000
  31.3 0.5 %copy.15 = f32[8]{0:T(128)} copy(f32[8]{0:T(128)S(1)} %bitcast.14) | data formatting | bytes 64
  31.9 0.6 %copy.16 = f32[250,8]{0,1:T(8,128)} copy(f32[250,8]{0,1:T(8,128)S(1)} %bitcast.9) | data formatting | bytes 16000
Async XLA Ops:
  0.6 1.6 %copy-start = (bf16[8,250,512]{2,0,1:T(8,128)(2,1)S(1)}, bf16[8,250,512]{2,0,1:T(8,128)(2,1)}, u32[]{:S(2)}) copy-start(bf16[8,250,512]{2,0,1:T(8,128)(2,1)} %param.5) | copy-start | bytes 6144004
  2.2 0.9 %copy-start.1 = (bf16[250,512]{1,0:T(8,128)(2,1)S(1)}, bf16[250,512]{1,0:T(8,128)(2,1)}, u32[]{:S(2)}) copy-start(bf16[250,512]{1,0:T(8,128)(2,1)} %outer_hbm.1) | copy-start | bytes 768004
  3.2 0.7 %copy-start.2 = (f32[512]{0:T(512)S(1)}, f32[512]{0:T(512)}, u32[]{:S(2)}) copy-start(f32[512]{0:T(512)} %param.9) | copy-start | bytes 6148
  3.8 0.7 %copy-start.3 = (f32[250]{0:T(256)S(1)}, f32[250]{0:T(256)}, u32[]{:S(2)}) copy-start(f32[250]{0:T(256)} %param.7) | copy-start | bytes 3004
  4.5 0.7 %copy-start.4 = (f32[250]{0:T(256)S(1)}, f32[250]{0:T(256)}, u32[]{:S(2)}) copy-start(f32[250]{0:T(256)} %param.8) | copy-start | bytes 3004

commit v2 on v1

--- a/solution.py
+++ b/solution.py
@@ -296,7 +296,7 @@
     tot[...] = whole
     totals = jnp.concatenate([whole[k : k + 1, :] for k in range(4)], axis=1)
     driver = driver_of(totals * (1.0 / inner))
-    rv_ref[...] = (
+    rv_ref[...] = jnp.zeros((1, 128), F32) + (
         jnp.sum(totals, axis=1, keepdims=True) * (1.0 / (M * inner))
         + jnp.sum(driver, axis=1, keepdims=True) * (1.0 / M)
     )
@@ -340,20 +340,25 @@
         ).wait_send()
 
 
+def hand_out(a, b, c, d, a_out, b_out, c_out, d_out, one, sem):
+    one[...] = a[0:1, 0:1]
+    pairs = ((d, d_out), (b, b_out), (c, c_out), (one, a_out))
+    copies = [pltpu.make_async_copy(src, dst, sem.at[k]) for k, (src, dst) in enumerate(pairs)]
+    for cp in copies:
+        cp.start()
+    for cp in copies:
+        cp.wait()
+
+
 def per_device(inner_noise, outer_noise, start, vol, times):
     K, D, M = inner_noise.shape
     hbm = pl.BlockSpec(memory_space=pltpu.HBM)
     vmem = pl.BlockSpec(memory_space=pltpu.VMEM)
     dma = pltpu.SemaphoreType.DMA
     V = pltpu.VMEM
-    root_value, root_grad, point_value, point_grad = pl.pallas_call(
+    results = pl.pallas_call(
         kernel,
-        out_shape=(
-            jax.ShapeDtypeStruct((1, 1), F32),
-            jax.ShapeDtypeStruct((1, D), F32),
-            jax.ShapeDtypeStruct((1, 8), F32),
-            jax.ShapeDtypeStruct((8, D), F32),
-        ),
+        out_shape=(V((1, 128), F32), V((1, D), F32), V((1, 8), F32), V((8, D), F32)),
         in_specs=[hbm] * 5,
         out_specs=(vmem,) * 4,
         scratch_shapes=[
@@ -368,11 +373,19 @@
             dma((NZ,)), dma((NZ,)), dma, dma, dma((3,)), dma((3,)), dma((7,)), dma((7,)),
         ],
         compiler_params=pltpu.CompilerParams(
-            collective_id=0, has_side_effects=True, vmem_limit_bytes=32 * 1024 * 1024
+            collective_id=0, has_side_effects=True
         ),
     )(
         jnp.transpose(inner_noise, (1, 0, 2)), outer_noise, start[None], vol[None], times[None]
     )
+    root_value, root_grad, point_value, point_grad = pl.pallas_call(
+        hand_out,
+        out_shape=tuple(jax.ShapeDtypeStruct(s, F32) for s in ((1, 1), (1, D), (1, 8), (8, D))),
+        in_specs=[vmem] * 4,
+        out_specs=(hbm,) * 4,
+        scratch_shapes=[V((1, 1), F32), dma((4,))],
+        compiler_params=pltpu.CompilerParams(vmem_limit_bytes=1024 * 1024),
+    )(*results)
     return root_value[0], root_grad[0], point_value[0], point_grad.T
 
 

time: 33.8 us -> 26.1 us (0.77)
  local copies, waits for them, and re-layouts: 6.23 us -> 0 us
  between operations: 2.34 us -> 0.64 us
  Pallas kernels: 25 us -> 25.4 us
    unnamed x13 -> x0, local copies, waits for them, and re-layouts: 6.23 us -> none
    pallas_call x1 -> x2, Pallas kernels: 25 us -> 25.4 us  [the longest x1 24.7 us: per_device(): pl.pallas_call(kernel, out_shape=(V((1, 128), F32), V((1, D), F32), V((1,...]
where the time goes in v2:
time: 26.1 us; the launch traced here: 26 us
  Pallas kernels  25.4 us (97%)
  between operations  0.64 us (2%)
    pallas_call x1, Pallas kernels, per_device(): pl.pallas_call(kernel, out_shape=(V((1, 128), F32), V((1, D), F32), V((1,...  24.7 us
    pallas_call x1, Pallas kernels, per_device(): pl.pallas_call(hand_out, out_shape=tuple((jax.ShapeDtypeStruct(s, F32) fo...  0.64 us

profile of v2, /device:TPU:1, one launch (start us, length us, event | category | flops | bytes accessed | tf_op | source)
XLA Modules:
  0.0 26.0 jit_solution(11927083859803329300)
XLA Ops:
  0.6 24.7 %shard_map.84 = (f32[1,128]{1,0:T(1,128)S(1)}, f32[1,250]{1,0:T(1,128)S(1)}, f32[1,8]{1,0:T(1,128)S(1)}, f32[8,250]{1,0:T(8,128)S(1)}) custom-call(bf16[250,8,512]{2,1,0:T(8,128)(2,1)} %bitcast.8, bf16[250,512]{1,0:T(8,128)(2,1)} %outer_hbm.1, f32[1,250]{1,0:T(1,128)} %bitcast.10, f32[1,250]{1,0:T(1,128)} %bitcast.11, f32[1,512]{1,0:T(1,128)} %bitcast.9), custom_call_target="tpu_custom_call" | custom-call | tf_op jit(solution)/shard_map/pallas_call | solution.py:359
  25.4 0.6 %shard_map.85 = (f32[1,1]{1,0:T(1,128)}, f32[1,250]{1,0:T(1,128)}, f32[1,8]{1,0:T(1,128)}, f32[8,250]{1,0:T(8,128)}) custom-call(f32[1,128]{1,0:T(1,128)S(1)} %get-tuple-element.12.a, f32[1,250]{1,0:T(1,128)S(1)} %get-tuple-element.13.b, f32[1,8]{1,0:T(1,128)S(1)} %get-tuple-element.14.c, f32[8,250]{1,0:T(8,128)S(1)} %get-tuple-element.15.d), custom_call_target="tpu_custom_call" | custom-call | tf_op jit(solution)/shard_map/pallas_call | solution.py:381

commit v3 on v2

--- a/solution.py
+++ b/solution.py
@@ -19,7 +19,6 @@
 MESH = pl.DeviceIdType.MESH
 F32 = jnp.float32
 BF16 = jnp.bfloat16
-CHUNKS = 5
 PAIRS = (2, 1, 3, 0)
 
 
@@ -33,10 +32,10 @@
     noise_hbm, outer_hbm, start_hbm, vol_hbm, times_hbm,
     rv_ref, rg_ref, pv_ref, pg_ref,
     noise, outer, start_v, vol_v, times_v,
-    startp, volp, volb, abase, lmin, rx, pay, stage, nt, rc, ry, rz, scm, smy, smz, tot, dinv,
-    in_sem, sx_s, sx_r, sc_s, sc_r, sy_s, sy_r, sz_s, sz_r, smc_s, smc_r, smy_s, smy_r, smz_s, smz_r,
+    startp, volp, volb, abase, lmin, rx, rtau, stage, nt, rc, ry, rz, smy, smz, tot, dinv,
+    in_sem, sx_s, sx_r, sc_s, sc_r, sy_s, sy_r, sz_s, sz_r, smy_s, smy_r, smz_s, smz_r, know,
 ):
-    D, K, M = noise.shape
+    D, K, M = noise_hbm.shape
     path = lax.axis_index("path")
     x = lax.axis_index("dim")
     z = path // (NY * NC)
@@ -51,13 +50,16 @@
         return ((zz * NY + yy) * NC + cc, x)
 
     barrier = pltpu.get_barrier_semaphore()
-    for k in range(1, NZ):
-        pl.semaphore_signal(barrier, inc=1, device_id=at((z + k) % NZ, y, c), device_id_type=MESH)
-    for k in range(1, NY):
-        pl.semaphore_signal(barrier, inc=1, device_id=at(z, (y + k) % NY, c), device_id_type=MESH)
-    for k in range(1, NX):
-        pl.semaphore_signal(barrier, inc=1, device_id=at_x(k), device_id_type=MESH)
-    pl.semaphore_signal(barrier, inc=1, device_id=at(z, y, 1 - c), device_id_type=MESH)
+    near = [at((z + k) % NZ, y, c) for k in (1, NZ - 1)]
+    near += [at(z, (y + k) % NY, cc) for k in (1, NY - 1) for cc in (c, 1 - c)]
+    near += [at_x(k) for k in (1, 2, 3)] + [at(z, y, 1 - c)]
+    for peer in near:
+        pl.semaphore_signal(barrier, inc=1, device_id=peer, device_id_type=MESH)
+
+    def tell(sem, peer):
+        pl.semaphore_signal(sem, inc=1, device_id=peer, device_id_type=MESH)
+
+    z_next, z_last = at((z + 1) % NZ, y, c), at((z + NZ - 1) % NZ, y, c)
 
     small_in = [
         pltpu.make_async_copy(vol_hbm, vol_v, in_sem.at[0]),
@@ -67,12 +69,12 @@
     ]
     for cp in small_in:
         cp.start()
-    per = D // CHUNKS
+    blocks = [(jz + off) % 4 for off in PAIRS]
     noise_in = [
         pltpu.make_async_copy(
-            noise_hbm.at[pl.ds(q * per, per)], noise.at[pl.ds(q * per, per)], in_sem.at[4 + q]
-        )
-        for q in range(CHUNKS)
+            noise_hbm.at[:, :, pl.ds(pl.multiple_of(j * 128, 128), 128)], noise.at[t], in_sem.at[4 + t]
+        )
+        for t, j in enumerate(blocks)
     ]
     for cp in noise_in:
         cp.start()
@@ -107,36 +109,38 @@
                 stage[lo:hi, :] + volb[lo:hi, :] * (root_t[:, ls] * o)
             ) * inv_root_tau[:, ls]
 
-    acc = tuple(jnp.full((K, 128), 3.0e38, F32) for _ in range(4))
+    def x_copy(t, k):
+        return pltpu.make_async_remote_copy(
+            src_ref=lmin.at[t], dst_ref=rx.at[k - 1, t],
+            send_sem=sx_s.at[t * 3 + k - 1], recv_sem=sx_r.at[t * 3 + k - 1],
+            device_id=at_x(k), device_id_type=MESH,
+        )
+
     unroll = 10
-    for q in range(CHUNKS):
-        noise_in[q].wait()
-
-        def body(g, acc, q=q):
-            acc = list(acc)
+    for t, j in enumerate(blocks):
+        noise_in[t].wait()
+
+        def body(g, acc, t=t, j=j):
+            terms = []
             for u in range(unroll):
-                d = q * per + g * unroll + u
-                v = volb[pl.ds(d, K, stride=0), :]
-                for j in range(4):
-                    n = noise[d, :, j * 128 : (j + 1) * 128].astype(F32)
-                    a = abase[j, pl.ds(d, K, stride=0), :]
-                    acc[j] = jnp.minimum(acc[j], n * v + a)
-            return tuple(acc)
-
-        acc = lax.fori_loop(0, per // unroll, body, acc)
-    for j in range(4):
-        lmin[:, j * 128 : (j + 1) * 128] = acc[j]
-
-    pl.semaphore_wait(barrier, (NZ - 1) + (NY - 1) + (NX - 1) + 1)
-
-    x_copies = []
-    for k in (2, 1, 3):
-        cp = pltpu.make_async_remote_copy(
-            src_ref=lmin, dst_ref=rx.at[k - 1], send_sem=sx_s.at[k - 1], recv_sem=sx_r.at[k - 1],
-            device_id=at_x(k), device_id_type=MESH,
-        )
-        cp.start()
-        x_copies.append(cp)
+                d = g * unroll + u
+                n = noise[t, d].astype(F32)
+                terms.append(
+                    n * volb[pl.ds(d, K, stride=0), :] + abase[j, pl.ds(d, K, stride=0), :]
+                )
+            while len(terms) > 1:
+                pairs = [jnp.minimum(a, b) for a, b in zip(terms[::2], terms[1::2])]
+                terms = pairs + terms[len(pairs) * 2 :]
+            return jnp.minimum(acc, terms[0])
+
+        lmin[t] = lax.fori_loop(0, D // unroll, body, jnp.full((K, 128), 3.0e38, F32))
+        if t == 0:
+            pl.semaphore_wait(barrier, len(near))
+            tell(know.at[0], at(z, (y + NY - 1) % NY, c))
+            tell(know.at[1], z_last)
+            tell(know.at[2], z_next)
+        for k in (2, 1, 3):
+            x_copy(t, k).start()
 
     lane = lax.broadcasted_iota(jnp.int32, (K, M), 1)
     row = lax.broadcasted_iota(jnp.int32, (K, M), 0)
@@ -152,12 +156,7 @@
     )
     dinv[...] = 1.0 / ((K * NZ * NY * NC) * vol_d * own_state * (1.0 - own_t))
 
-    for cp in x_copies:
-        cp.wait_recv()
-    least = jnp.minimum(jnp.minimum(lmin[...], rx[0]), jnp.minimum(rx[1], rx[2]))
-    payoff = jnp.exp(root_tau * least)
-    pay[...] = payoff * root_tau
-    totals = jnp.sum(payoff, axis=0, keepdims=True)
+    rtau[...] = root_tau
 
     sub = lax.broadcasted_iota(jnp.int32, (8, 128), 0)
     bit2 = (sub & 4) == 0
@@ -178,6 +177,12 @@
         e2 = [merge(c4[s], c4[s + 2], bit1, 2) for s in range(2)]
         return merge(e2[0], e2[1], bit0, 1)
 
+    pl.semaphore_wait(know.at[0], 1)
+    pl.semaphore_wait(know.at[1], 1)
+    pl.semaphore_wait(know.at[2], 1)
+    tell(know.at[3], z_last)
+    tell(know.at[4], z_next)
+
     def core_copy(t):
         return pltpu.make_async_remote_copy(
             src_ref=nt.at[t, 1 - c], dst_ref=rc.at[t], send_sem=sc_s.at[t], recv_sem=sc_r.at[t],
@@ -200,18 +205,34 @@
 
     wsum = jnp.zeros((8, 256), F32)
     full = D // 8
-    for t, off in enumerate(PAIRS):
-        j = (jz + off) % 4
+    small_y = []
+    tot[...] = jnp.zeros_like(tot)
+    for t, j in enumerate(blocks):
+        for k in (1, 2, 3):
+            x_copy(t, k).wait_recv()
         lanes = pl.ds(pl.multiple_of(j * 128, 128), 128)
-        p = pay[:, lanes]
-
-        def group(g, _, p=p, lanes=lanes):
-            ys = [noise[g * 8 + s, :, lanes].astype(F32) * p for s in range(8)]
-            stage[pl.ds(pl.multiple_of(g * 8, 8), 8), :] = sums_of(ys)
+        least = jnp.minimum(
+            jnp.minimum(lmin[t], rx[0, t]), jnp.minimum(rx[1, t], rx[2, t])
+        )
+        scale = rtau[:, lanes]
+        payoff = jnp.exp(scale * least)
+        p = payoff * scale
+        tot[pl.ds(j, 1), :] = jnp.sum(payoff, axis=0, keepdims=True)
+
+        def group(g, t=t, p=p):
+            ys = [noise[t, g * 8 + s].astype(F32) * p for s in range(8)]
+            return sums_of(ys)
+
+        def groups(r, _, group=group):
+            for u in range(6):
+                g = r * 6 + u
+                stage[pl.ds(pl.multiple_of(g * 8, 8), 8), :] = group(g)
             return 0
 
-        lax.fori_loop(0, full, group, 0)
-        rest = [noise[full * 8 + s, :, lanes].astype(F32) * p for s in range(D - full * 8)]
+        lax.fori_loop(0, full // 6, groups, 0)
+        for g in range(full // 6 * 6, full):
+            stage[g * 8 : g * 8 + 8, :] = group(g)
+        rest = [noise[t, full * 8 + s].astype(F32) * p for s in range(D - full * 8)]
         rest += [jnp.zeros((8, 128), F32)] * (8 - len(rest))
         stage[full * 8 : full * 8 + 8, :] = sums_of(rest)
         for h in range(2):
@@ -227,32 +248,28 @@
                 if h == 0
                 else jnp.concatenate([jnp.zeros((8, 128), F32), part], axis=1)
             )
+        if t == 0:
+            pl.semaphore_wait(know.at[3], 1)
+            pl.semaphore_wait(know.at[4], 1)
+            tell(know.at[5], z_last)
         if t == 3:
             w = jnp.sum(wsum, axis=0, keepdims=True)
-            scm[0] = jnp.concatenate(
-                [totals[:, k * 128 : (k + 1) * 128] for k in range(4)]
-                + [w[:, 0:128], w[:, 128:256], jnp.zeros((2, 128), F32)],
-                axis=0,
-            )
-            small_core = pltpu.make_async_remote_copy(
-                src_ref=scm.at[0], dst_ref=scm.at[1], send_sem=smc_s, recv_sem=smc_r,
-                device_id=at(z, y, 1 - c), device_id_type=MESH,
-            )
-            small_core.start()
+            tot[4:5, :] = w[:, 0:128]
+            tot[5:6, :] = w[:, 128:256]
+            me = y * NC + c
+            smy[me] = tot[...]
+            for k in (4, 5, 3, 2, 7, 6, 1):
+                cp = pltpu.make_async_remote_copy(
+                    src_ref=smy.at[me], dst_ref=smy.at[me], send_sem=smy_s.at[k - 1], recv_sem=smy_r.at[k - 1],
+                    device_id=at(z, (y + k // 2) % NY, (c + k) % 2), device_id_type=MESH,
+                )
+                cp.start()
+                small_y.append(cp)
         core_copy(t).start()
         if t >= 1:
             after_core(t - 1)
 
-    small_core.wait_recv()
-    smy[y] = scm[0] + scm[1]
-    small_y = []
-    for k in (2, 1, 3):
-        cp = pltpu.make_async_remote_copy(
-            src_ref=smy.at[y], dst_ref=smy.at[y], send_sem=smy_s.at[k - 1], recv_sem=smy_r.at[k - 1],
-            device_id=at(z, (y + k) % NY, c), device_id_type=MESH,
-        )
-        cp.start()
-        small_y.append(cp)
+    pl.semaphore_wait(know.at[5], 1)
     after_core(3)
 
     def z_copy(t, peer, zz):
@@ -276,7 +293,7 @@
     after_y(0)
     for cp in small_y:
         cp.wait_recv()
-    smz[z] = (smy[0] + smy[1]) + (smy[2] + smy[3])
+    smz[z] = ((smy[0] + smy[1]) + (smy[2] + smy[3])) + ((smy[4] + smy[5]) + (smy[6] + smy[7]))
     small_z = []
     for k in (4, 3, 5, 2, 6, 1, 7):
         cp = pltpu.make_async_remote_copy(
@@ -326,10 +343,12 @@
         own = own + rz[src]
     pg_ref[...] = own[:, 0:D] * dinv[...]
 
-    for cp in x_copies + small_y + small_z + [small_core]:
+    for cp in small_y + small_z:
         cp.wait_send()
     for t in range(4):
         core_copy(t).wait_send()
+        for k in (1, 2, 3):
+            x_copy(t, k).wait_send()
         for k in range(1, NY):
             y_copy(t, k).wait_send()
     for k in range(1, NZ):
@@ -362,15 +381,16 @@
         in_specs=[hbm] * 5,
         out_specs=(vmem,) * 4,
         scratch_shapes=[
-            V((D, K, M), BF16), V((D, M), BF16), V((1, D), F32), V((1, D), F32), V((1, M), F32),
+            V((4, D, K, 128), BF16), V((D, M), BF16), V((1, D), F32), V((1, D), F32), V((1, M), F32),
             V((1, 256), F32), V((1, 256), F32), V((256, 128), F32), V((4, 256, 128), F32),
-            V((K, M), F32), V((3, K, M), F32), V((K, M), F32), V((256, 128), F32),
+            V((4, K, 128), F32), V((3, 4, K, 128), F32), V((1, M), F32), V((256, 128), F32),
             V((4, NC, NY, 2, 8, 256), F32), V((4, NY, 2, 8, 256), F32),
             V((4, 3, 2, 8, 256), F32), V((NZ, 8, 256), F32),
-            V((2, 8, 128), F32), V((NY, 8, 128), F32), V((NZ, 8, 128), F32), V((8, 128), F32),
+            V((NY * NC, 8, 128), F32), V((NZ, 8, 128), F32), V((8, 128), F32),
             V((8, D), F32),
-            dma((4 + CHUNKS,)), dma((3,)), dma((3,)), dma((4,)), dma((4,)), dma((12,)), dma((12,)),
-            dma((NZ,)), dma((NZ,)), dma, dma, dma((3,)), dma((3,)), dma((7,)), dma((7,)),
+            dma((8,)), dma((12,)), dma((12,)), dma((4,)), dma((4,)), dma((12,)), dma((12,)),
+            dma((NZ,)), dma((NZ,)), dma((7,)), dma((7,)), dma((7,)), dma((7,)),
+            pltpu.SemaphoreType.REGULAR((6,)),
         ],
         compiler_params=pltpu.CompilerParams(
             collective_id=0, has_side_effects=True

time: 26.1 us -> 25.2 us (0.966)
  Pallas kernels: 25.4 us -> 24.5 us
    pallas_call x1, Pallas kernels: 24.7 us -> 23.8 us  [per_device(): pl.pallas_call(kernel, out_shape=(V((1, 128), F32), V((1, D), F32), V((1,...]
where the time goes in v3:
time: 25.2 us; the launch traced here: 25.1 us
  Pallas kernels  24.5 us (97%)
  between operations  0.64 us (3%)
    pallas_call x1, Pallas kernels, per_device(): pl.pallas_call(kernel, out_shape=(V((1, 128), F32), V((1, D), F32), V((1,...  23.8 us
    pallas_call x1, Pallas kernels, per_device(): pl.pallas_call(hand_out, out_shape=tuple((jax.ShapeDtypeStruct(s, F32) fo...  0.64 us

profile of v3, /device:TPU:1, one launch (start us, length us, event | category | flops | bytes accessed | tf_op | source)
XLA Modules:
  0.0 25.1 jit_solution(14880572860444420736)
XLA Ops:
  0.6 23.8 %shard_map.84 = (f32[1,128]{1,0:T(1,128)S(1)}, f32[1,250]{1,0:T(1,128)S(1)}, f32[1,8]{1,0:T(1,128)S(1)}, f32[8,250]{1,0:T(8,128)S(1)}) custom-call(bf16[250,8,512]{2,1,0:T(8,128)(2,1)} %bitcast.8, bf16[250,512]{1,0:T(8,128)(2,1)} %outer_hbm.1, f32[1,250]{1,0:T(1,128)} %bitcast.10, f32[1,250]{1,0:T(1,128)} %bitcast.11, f32[1,512]{1,0:T(1,128)} %bitcast.9), custom_call_target="tpu_custom_call" | custom-call | tf_op jit(solution)/shard_map/pallas_call | solution.py:378
  24.5 0.6 %shard_map.85 = (f32[1,1]{1,0:T(1,128)}, f32[1,250]{1,0:T(1,128)}, f32[1,8]{1,0:T(1,128)}, f32[8,250]{1,0:T(8,128)}) custom-call(f32[1,128]{1,0:T(1,128)S(1)} %get-tuple-element.12.a, f32[1,250]{1,0:T(1,128)S(1)} %get-tuple-element.13.b, f32[1,8]{1,0:T(1,128)S(1)} %get-tuple-element.14.c, f32[8,250]{1,0:T(8,128)S(1)} %get-tuple-element.15.d), custom_call_target="tpu_custom_call" | custom-call | tf_op jit(solution)/shard_map/pallas_call | solution.py:401

commit v4 on v3

--- a/solution.py
+++ b/solution.py
@@ -26,6 +26,13 @@
     slope = jnp.clip((value - value_high) / (value_low - value_high), 0.0, 1.0)
     quota = gamma_high + (gamma_low - gamma_high) * slope
     return -(1.0 - delta) * quota * value - rate_free * value
+
+
+def smallest(terms):
+    while len(terms) > 1:
+        pairs = [jnp.minimum(a, b) for a, b in zip(terms[::2], terms[1::2])]
+        terms = pairs + terms[len(pairs) * 2 :]
+    return terms[0]
 
 
 def kernel(
@@ -49,18 +56,6 @@
     def at(zz, yy, cc):
         return ((zz * NY + yy) * NC + cc, x)
 
-    barrier = pltpu.get_barrier_semaphore()
-    near = [at((z + k) % NZ, y, c) for k in (1, NZ - 1)]
-    near += [at(z, (y + k) % NY, cc) for k in (1, NY - 1) for cc in (c, 1 - c)]
-    near += [at_x(k) for k in (1, 2, 3)] + [at(z, y, 1 - c)]
-    for peer in near:
-        pl.semaphore_signal(barrier, inc=1, device_id=peer, device_id_type=MESH)
-
-    def tell(sem, peer):
-        pl.semaphore_signal(sem, inc=1, device_id=peer, device_id_type=MESH)
-
-    z_next, z_last = at((z + 1) % NZ, y, c), at((z + NZ - 1) % NZ, y, c)
-
     small_in = [
         pltpu.make_async_copy(vol_hbm, vol_v, in_sem.at[0]),
         pltpu.make_async_copy(start_hbm, start_v, in_sem.at[1]),
@@ -78,6 +73,18 @@
     ]
     for cp in noise_in:
         cp.start()
+    barrier = pltpu.get_barrier_semaphore()
+    near = [at((z + k) % NZ, y, c) for k in (1, NZ - 1)]
+    near += [at(z, (y + k) % NY, cc) for k in (1, NY - 1) for cc in (c, 1 - c)]
+    near += [at_x(k) for k in (1, 2, 3)] + [at(z, y, 1 - c)]
+    for peer in near:
+        pl.semaphore_signal(barrier, inc=1, device_id=peer, device_id_type=MESH)
+
+    def tell(sem, peer):
+        pl.semaphore_signal(sem, inc=1, device_id=peer, device_id_type=MESH)
+
+    z_next, z_last = at((z + 1) % NZ, y, c), at((z + NZ - 1) % NZ, y, c)
+
     for cp in small_in:
         cp.wait()
 
@@ -116,31 +123,31 @@
             device_id=at_x(k), device_id_type=MESH,
         )
 
-    unroll = 10
-    for t, j in enumerate(blocks):
+    unroll = 25
+    for t in (0, 2):
         noise_in[t].wait()
-
-        def body(g, acc, t=t, j=j):
-            terms = []
+        noise_in[t + 1].wait()
+
+        def body(g, acc, t=t):
+            terms = [[], []]
             for u in range(unroll):
                 d = g * unroll + u
-                n = noise[t, d].astype(F32)
-                terms.append(
-                    n * volb[pl.ds(d, K, stride=0), :] + abase[j, pl.ds(d, K, stride=0), :]
-                )
-            while len(terms) > 1:
-                pairs = [jnp.minimum(a, b) for a, b in zip(terms[::2], terms[1::2])]
-                terms = pairs + terms[len(pairs) * 2 :]
-            return jnp.minimum(acc, terms[0])
-
-        lmin[t] = lax.fori_loop(0, D // unroll, body, jnp.full((K, 128), 3.0e38, F32))
+                v = volb[pl.ds(d, K, stride=0), :]
+                for h in range(2):
+                    n = noise[t + h, d].astype(F32)
+                    terms[h].append(n * v + abase[blocks[t + h], pl.ds(d, K, stride=0), :])
+            return tuple(jnp.minimum(a, smallest(r)) for a, r in zip(acc, terms))
+
+        acc = lax.fori_loop(0, D // unroll, body, (jnp.full((K, 128), 3.0e38, F32),) * 2)
+        lmin[t], lmin[t + 1] = acc
         if t == 0:
             pl.semaphore_wait(barrier, len(near))
             tell(know.at[0], at(z, (y + NY - 1) % NY, c))
             tell(know.at[1], z_last)
             tell(know.at[2], z_next)
-        for k in (2, 1, 3):
-            x_copy(t, k).start()
+        for h in range(2):
+            for k in (2, 1, 3):
+                x_copy(t + h, k).start()
 
     lane = lax.broadcasted_iota(jnp.int32, (K, M), 1)
     row = lax.broadcasted_iota(jnp.int32, (K, M), 0)
@@ -266,10 +273,9 @@
                 cp.start()
                 small_y.append(cp)
         core_copy(t).start()
-        if t >= 1:
-            after_core(t - 1)
-
-    pl.semaphore_wait(know.at[5], 1)
+
+    for t in range(3):
+        after_core(t)
     after_core(3)
 
     def z_copy(t, peer, zz):
@@ -290,7 +296,7 @@
             for zz in range(2):
                 z_copy(t, base + zz, zz).start()
 
-    after_y(0)
+    pl.semaphore_wait(know.at[5], 1)
     for cp in small_y:
         cp.wait_recv()
     smz[z] = ((smy[0] + smy[1]) + (smy[2] + smy[3])) + ((smy[4] + smy[5]) + (smy[6] + smy[7]))
@@ -302,6 +308,7 @@
         )
         cp.start()
         small_z.append(cp)
+    after_y(0)
     after_y(1)
     after_y(2)
     after_y(3)

time: 25.2 us -> 24.5 us (0.972)
  Pallas kernels: 24.5 us -> 23.7 us
    pallas_call x1, Pallas kernels: 23.8 us -> 23.1 us  [per_device(): pl.pallas_call(kernel, out_shape=(V((1, 128), F32), V((1, D), F32), V((1,...]
where the time goes in v4:
time: 24.5 us; the launch traced here: 24.3 us
  Pallas kernels  23.7 us (97%)
  between operations  0.64 us (3%)
    pallas_call x1, Pallas kernels, per_device(): pl.pallas_call(kernel, out_shape=(V((1, 128), F32), V((1, D), F32), V((1,...  23.1 us
    pallas_call x1, Pallas kernels, per_device(): pl.pallas_call(hand_out, out_shape=tuple((jax.ShapeDtypeStruct(s, F32) fo...  0.64 us

profile of v4, /device:TPU:1, one launch (start us, length us, event | category | flops | bytes accessed | tf_op | source)
XLA Modules:
  0.0 24.3 jit_solution(3230623250757652589)
XLA Ops:
  0.6 23.1 %shard_map.84 = (f32[1,128]{1,0:T(1,128)S(1)}, f32[1,250]{1,0:T(1,128)S(1)}, f32[1,8]{1,0:T(1,128)S(1)}, f32[8,250]{1,0:T(8,128)S(1)}) custom-call(bf16[250,8,512]{2,1,0:T(8,128)(2,1)} %bitcast.8, bf16[250,512]{1,0:T(8,128)(2,1)} %outer_hbm.1, f32[1,250]{1,0:T(1,128)} %bitcast.10, f32[1,250]{1,0:T(1,128)} %bitcast.11, f32[1,512]{1,0:T(1,128)} %bitcast.9), custom_call_target="tpu_custom_call" | custom-call | tf_op jit(solution)/shard_map/pallas_call | solution.py:385
  23.7 0.6 %shard_map.85 = (f32[1,1]{1,0:T(1,128)}, f32[1,250]{1,0:T(1,128)}, f32[1,8]{1,0:T(1,128)}, f32[8,250]{1,0:T(8,128)}) custom-call(f32[1,128]{1,0:T(1,128)S(1)} %get-tuple-element.12.a, f32[1,250]{1,0:T(1,128)S(1)} %get-tuple-element.13.b, f32[1,8]{1,0:T(1,128)S(1)} %get-tuple-element.14.c, f32[8,250]{1,0:T(8,128)S(1)} %get-tuple-element.15.d), custom_call_target="tpu_custom_call" | custom-call | tf_op jit(solution)/shard_map/pallas_call | solution.py:408

commit v5 on v4

--- a/solution.py
+++ b/solution.py
@@ -19,7 +19,7 @@
 MESH = pl.DeviceIdType.MESH
 F32 = jnp.float32
 BF16 = jnp.bfloat16
-PAIRS = (2, 1, 3, 0)
+CHUNKS = 5
 
 
 def driver_of(value):
@@ -39,7 +39,7 @@
     noise_hbm, outer_hbm, start_hbm, vol_hbm, times_hbm,
     rv_ref, rg_ref, pv_ref, pg_ref,
     noise, outer, start_v, vol_v, times_v,
-    startp, volp, volb, abase, lmin, rx, rtau, stage, nt, rc, ry, rz, smy, smz, tot, dinv,
+    startp, volp, volb, abase, lmin, rx, rows_t, stage, nt, rc, ry, rz, smy, smz, tot, dinv,
     in_sem, sx_s, sx_r, sc_s, sc_r, sy_s, sy_r, sz_s, sz_r, smy_s, smy_r, smz_s, smz_r, know,
 ):
     D, K, M = noise_hbm.shape
@@ -60,19 +60,34 @@
         pltpu.make_async_copy(vol_hbm, vol_v, in_sem.at[0]),
         pltpu.make_async_copy(start_hbm, start_v, in_sem.at[1]),
         pltpu.make_async_copy(times_hbm, times_v, in_sem.at[2]),
-        pltpu.make_async_copy(outer_hbm, outer, in_sem.at[3]),
     ]
     for cp in small_in:
         cp.start()
-    blocks = [(jz + off) % 4 for off in PAIRS]
+    odd = z % 2
+    blocks = [(jz + off) % 4 for off in (2, 1 + 2 * odd, 3 - 2 * odd, 0)]
+
+    def lanes_of(t):
+        return pl.ds(pl.multiple_of(blocks[t] * 128, 128), 128)
+
+    per = D // CHUNKS
+    outer_in = [
+        pltpu.make_async_copy(outer_hbm.at[:, lanes_of(t)], outer.at[:, lanes_of(t)], in_sem.at[3 + t])
+        for t in range(4)
+    ]
     noise_in = [
-        pltpu.make_async_copy(
-            noise_hbm.at[:, :, pl.ds(pl.multiple_of(j * 128, 128), 128)], noise.at[t], in_sem.at[4 + t]
-        )
-        for t, j in enumerate(blocks)
+        [
+            pltpu.make_async_copy(
+                noise_hbm.at[pl.ds(q * per, per), :, lanes_of(t)],
+                noise.at[t, pl.ds(q * per, per)],
+                in_sem.at[7 + t * CHUNKS + q],
+            )
+            for q in range(CHUNKS)
+        ]
+        for t in range(4)
     ]
-    for cp in noise_in:
+    for cp in [outer_in[0]] + noise_in[0]:
         cp.start()
+
     barrier = pltpu.get_barrier_semaphore()
     near = [at((z + k) % NZ, y, c) for k in (1, NZ - 1)]
     near += [at(z, (y + k) % NY, cc) for k in (1, NY - 1) for cc in (c, 1 - c)]
@@ -85,6 +100,9 @@
 
     z_next, z_last = at((z + 1) % NZ, y, c), at((z + NZ - 1) % NZ, y, c)
 
+    for t in range(1, 4):
+        for cp in [outer_in[t]] + noise_in[t]:
+            cp.start()
     for cp in small_in:
         cp.wait()
 
@@ -107,14 +125,18 @@
         stage[h * 128 : (h + 1) * 128, :] = jnp.broadcast_to(
             offset[:, h * 128 : (h + 1) * 128], (128, 128)
         ).T
-    for lo in range(0, D, 16):
-        hi = min(lo + 16, D)
-        for j in range(4):
-            ls = slice(j * 128, (j + 1) * 128)
-            o = outer[lo:hi, ls].astype(F32)
-            abase[j, lo:hi, :] = (
-                stage[lo:hi, :] + volb[lo:hi, :] * (root_t[:, ls] * o)
-            ) * inv_root_tau[:, ls]
+    rows_t[0:1, :] = root_t
+    rows_t[1:2, :] = root_tau
+    rows_t[2:3, :] = inv_root_tau
+
+    def coefficients(t):
+        outer_in[t].wait()
+        scale = rows_t[0:1, lanes_of(t)]
+        inv = rows_t[2:3, lanes_of(t)]
+        for lo in range(0, D, 16):
+            hi = min(lo + 16, D)
+            o = outer[lo:hi, lanes_of(t)].astype(F32)
+            abase[t, lo:hi, :] = (stage[lo:hi, :] + volb[lo:hi, :] * (scale * o)) * inv
 
     def x_copy(t, k):
         return pltpu.make_async_remote_copy(
@@ -123,31 +145,32 @@
             device_id=at_x(k), device_id_type=MESH,
         )
 
-    unroll = 25
-    for t in (0, 2):
-        noise_in[t].wait()
-        noise_in[t + 1].wait()
-
-        def body(g, acc, t=t):
-            terms = [[], []]
-            for u in range(unroll):
-                d = g * unroll + u
+    def minimum_of(ts):
+        acc = [jnp.full((K, 128), 3.0e38, F32) for _ in ts]
+        for q in range(CHUNKS):
+            terms = [[] for _ in ts]
+            for t in ts:
+                noise_in[t][q].wait()
+            for d in range(q * per, (q + 1) * per):
                 v = volb[pl.ds(d, K, stride=0), :]
-                for h in range(2):
-                    n = noise[t + h, d].astype(F32)
-                    terms[h].append(n * v + abase[blocks[t + h], pl.ds(d, K, stride=0), :])
-            return tuple(jnp.minimum(a, smallest(r)) for a, r in zip(acc, terms))
-
-        acc = lax.fori_loop(0, D // unroll, body, (jnp.full((K, 128), 3.0e38, F32),) * 2)
-        lmin[t], lmin[t + 1] = acc
-        if t == 0:
+                for row, t in zip(terms, ts):
+                    row.append(noise[t, d].astype(F32) * v + abase[t, pl.ds(d, K, stride=0), :])
+            acc = [jnp.minimum(a, smallest(r)) for a, r in zip(acc, terms)]
+        for t, a in zip(ts, acc):
+            lmin[t] = a
+
+    for ts in ((0,), (1,), (2, 3)):
+        for t in ts:
+            coefficients(t)
+        minimum_of(ts)
+        if ts[0] == 0:
             pl.semaphore_wait(barrier, len(near))
             tell(know.at[0], at(z, (y + NY - 1) % NY, c))
             tell(know.at[1], z_last)
             tell(know.at[2], z_next)
-        for h in range(2):
+        for t in ts:
             for k in (2, 1, 3):
-                x_copy(t + h, k).start()
+                x_copy(t, k).start()
 
     lane = lax.broadcasted_iota(jnp.int32, (K, M), 1)
     row = lax.broadcasted_iota(jnp.int32, (K, M), 0)
@@ -163,8 +186,6 @@
     )
     dinv[...] = 1.0 / ((K * NZ * NY * NC) * vol_d * own_state * (1.0 - own_t))
 
-    rtau[...] = root_tau
-
     sub = lax.broadcasted_iota(jnp.int32, (8, 128), 0)
     bit2 = (sub & 4) == 0
     bit1 = (sub & 2) == 0
@@ -210,59 +231,41 @@
         for k in (2, 1, 3):
             y_copy(t, k).start()
 
-    wsum = jnp.zeros((8, 256), F32)
-    full = D // 8
+    wsum = [jnp.zeros((8, 128), F32)] * 2
     small_y = []
     tot[...] = jnp.zeros_like(tot)
     for t, j in enumerate(blocks):
         for k in (1, 2, 3):
             x_copy(t, k).wait_recv()
-        lanes = pl.ds(pl.multiple_of(j * 128, 128), 128)
         least = jnp.minimum(
             jnp.minimum(lmin[t], rx[0, t]), jnp.minimum(rx[1, t], rx[2, t])
         )
-        scale = rtau[:, lanes]
+        scale = rows_t[1:2, lanes_of(t)]
         payoff = jnp.exp(scale * least)
         p = payoff * scale
         tot[pl.ds(j, 1), :] = jnp.sum(payoff, axis=0, keepdims=True)
-
-        def group(g, t=t, p=p):
-            ys = [noise[t, g * 8 + s].astype(F32) * p for s in range(8)]
-            return sums_of(ys)
-
-        def groups(r, _, group=group):
-            for u in range(6):
-                g = r * 6 + u
-                stage[pl.ds(pl.multiple_of(g * 8, 8), 8), :] = group(g)
-            return 0
-
-        lax.fori_loop(0, full // 6, groups, 0)
-        for g in range(full // 6 * 6, full):
-            stage[g * 8 : g * 8 + 8, :] = group(g)
-        rest = [noise[t, full * 8 + s].astype(F32) * p for s in range(D - full * 8)]
-        rest += [jnp.zeros((8, 128), F32)] * (8 - len(rest))
-        stage[full * 8 : full * 8 + 8, :] = sums_of(rest)
         for h in range(2):
-            block = stage[h * 128 : (h + 1) * 128, :].T
+            tiles = []
+            for g in range(16):
+                first = h * 128 + g * 8
+                ys = [noise[t, first + s].astype(F32) * p for s in range(min(8, D - first))]
+                ys += [jnp.zeros((8, 128), F32)] * (8 - len(ys))
+                tiles.append(sums_of(ys))
+            block = jnp.concatenate(tiles, axis=0).T
             part = jnp.zeros((8, 128), F32)
             for q in range(16):
                 zz, yy, cc = q // 8, (q // 2) % 4, q % 2
                 piece = block[q * 8 : (q + 1) * 8, :]
                 nt[t, cc, yy, zz, :, h * 128 : (h + 1) * 128] = piece
                 part = part + piece
-            wsum = wsum + (
-                jnp.concatenate([part, jnp.zeros((8, 128), F32)], axis=1)
-                if h == 0
-                else jnp.concatenate([jnp.zeros((8, 128), F32), part], axis=1)
-            )
+            wsum[h] = wsum[h] + part
         if t == 0:
             pl.semaphore_wait(know.at[3], 1)
             pl.semaphore_wait(know.at[4], 1)
             tell(know.at[5], z_last)
         if t == 3:
-            w = jnp.sum(wsum, axis=0, keepdims=True)
-            tot[4:5, :] = w[:, 0:128]
-            tot[5:6, :] = w[:, 128:256]
+            for h in range(2):
+                tot[4 + h : 5 + h, :] = jnp.sum(wsum[h], axis=0, keepdims=True)
             me = y * NC + c
             smy[me] = tot[...]
             for k in (4, 5, 3, 2, 7, 6, 1):
@@ -288,10 +291,9 @@
         for k in range(1, NY):
             y_copy(t, k).wait_recv()
         nt[t, c, y] = nt[t, c, y] + (ry[t, 0] + ry[t, 1] + ry[t, 2])
-        base = 2 * ((jz + PAIRS[t]) % 4)
-        if PAIRS[t] == 0:
-            peer = base + 1 - z % 2
-            z_copy(t, peer, 1 - z % 2).start()
+        base = 2 * blocks[t]
+        if t == 3:
+            z_copy(t, base + 1 - odd, 1 - odd).start()
         else:
             for zz in range(2):
                 z_copy(t, base + zz, zz).start()
@@ -340,7 +342,7 @@
     own_row = pltpu.roll(jnp.broadcast_to(own_row, (8, 128)), (128 - (path % 16) * 8) % 128, axis=1)
     pv_ref[...] = own_row[0:1, 0:8]
 
-    own = nt[3, c, y, z % 2]
+    own = nt[3, c, y, odd]
     for k in range(1, NZ):
         src = (z + k) % NZ
         pltpu.make_async_remote_copy(
@@ -390,12 +392,12 @@
         scratch_shapes=[
             V((4, D, K, 128), BF16), V((D, M), BF16), V((1, D), F32), V((1, D), F32), V((1, M), F32),
             V((1, 256), F32), V((1, 256), F32), V((256, 128), F32), V((4, 256, 128), F32),
-            V((4, K, 128), F32), V((3, 4, K, 128), F32), V((1, M), F32), V((256, 128), F32),
+            V((4, K, 128), F32), V((3, 4, K, 128), F32), V((8, M), F32), V((256, 128), F32),
             V((4, NC, NY, 2, 8, 256), F32), V((4, NY, 2, 8, 256), F32),
             V((4, 3, 2, 8, 256), F32), V((NZ, 8, 256), F32),
             V((NY * NC, 8, 128), F32), V((NZ, 8, 128), F32), V((8, 128), F32),
             V((8, D), F32),
-            dma((8,)), dma((12,)), dma((12,)), dma((4,)), dma((4,)), dma((12,)), dma((12,)),
+            dma((7 + 4 * CHUNKS,)), dma((12,)), dma((12,)), dma((4,)), dma((4,)), dma((12,)), dma((12,)),
             dma((NZ,)), dma((NZ,)), dma((7,)), dma((7,)), dma((7,)), dma((7,)),
             pltpu.SemaphoreType.REGULAR((6,)),
         ],

time: 24.5 us -> 24.5 us (level)
  no operation moved by 1% of the time
where the time goes in v5:
time: 24.5 us; the launch traced here: 24.4 us
  Pallas kernels  23.7 us (97%)
  between operations  0.64 us (3%)
    pallas_call x1, Pallas kernels, per_device(): pl.pallas_call(kernel, out_shape=(V((1, 128), F32), V((1, D), F32), V((1,...  23.1 us
    pallas_call x1, Pallas kernels, per_device(): pl.pallas_call(hand_out, out_shape=tuple((jax.ShapeDtypeStruct(s, F32) fo...  0.64 us

profile of v5, /device:TPU:1, one launch (start us, length us, event | category | flops | bytes accessed | tf_op | source)
XLA Modules:
  0.0 24.4 jit_solution(558259363992427452)
XLA Ops:
  0.6 23.1 %shard_map.84 = (f32[1,128]{1,0:T(1,128)S(1)}, f32[1,250]{1,0:T(1,128)S(1)}, f32[1,8]{1,0:T(1,128)S(1)}, f32[8,250]{1,0:T(8,128)S(1)}) custom-call(bf16[250,8,512]{2,1,0:T(8,128)(2,1)} %bitcast.8, bf16[250,512]{1,0:T(8,128)(2,1)} %outer_hbm.1, f32[1,250]{1,0:T(1,128)} %bitcast.10, f32[1,250]{1,0:T(1,128)} %bitcast.11, f32[1,512]{1,0:T(1,128)} %bitcast.9), custom_call_target="tpu_custom_call" | custom-call | tf_op jit(solution)/shard_map/pallas_call | solution.py:387
  23.7 0.6 %shard_map.85 = (f32[1,1]{1,0:T(1,128)}, f32[1,250]{1,0:T(1,128)}, f32[1,8]{1,0:T(1,128)}, f32[8,250]{1,0:T(8,128)}) custom-call(f32[1,128]{1,0:T(1,128)S(1)} %get-tuple-element.12.a, f32[1,250]{1,0:T(1,128)S(1)} %get-tuple-element.13.b, f32[1,8]{1,0:T(1,128)S(1)} %get-tuple-element.14.c, f32[8,250]{1,0:T(8,128)S(1)} %get-tuple-element.15.d), custom_call_target="tpu_custom_call" | custom-call | tf_op jit(solution)/shard_map/pallas_call | solution.py:410

commit v6 on v5

--- a/solution.py
+++ b/solution.py
@@ -38,9 +38,9 @@
 def kernel(
     noise_hbm, outer_hbm, start_hbm, vol_hbm, times_hbm,
     rv_ref, rg_ref, pv_ref, pg_ref,
-    noise, outer, start_v, vol_v, times_v,
-    startp, volp, volb, abase, lmin, rx, rows_t, stage, nt, rc, ry, rz, smy, smz, tot, dinv,
-    in_sem, sx_s, sx_r, sc_s, sc_r, sy_s, sy_r, sz_s, sz_r, smy_s, smy_r, smz_s, smz_r, know,
+    noise, turned, outer, start_v, vol_v, times_v,
+    startp, volp, volb, abase, lmin, rx, rows_t, stage, nt, rc, ry, rz, rf, far_sum, bytes_of, smy, smz, tot, dinv,
+    in_sem, sent, x_in, core_in, y_in, z_in, far_z_in, far_y_in, small_y_in, small_z_in, know,
 ):
     D, K, M = noise_hbm.shape
     path = lax.axis_index("path")
@@ -79,7 +79,7 @@
             pltpu.make_async_copy(
                 noise_hbm.at[pl.ds(q * per, per), :, lanes_of(t)],
                 noise.at[t, pl.ds(q * per, per)],
-                in_sem.at[7 + t * CHUNKS + q],
+                in_sem.at[7 + t],
             )
             for q in range(CHUNKS)
         ]
@@ -103,6 +103,8 @@
     for t in range(1, 4):
         for cp in [outer_in[t]] + noise_in[t]:
             cp.start()
+    for t in range(4):
+        noise[t, D:] = jnp.zeros((256 - D, K, 128), BF16)
     for cp in small_in:
         cp.wait()
 
@@ -138,19 +140,22 @@
             o = outer[lo:hi, lanes_of(t)].astype(F32)
             abase[t, lo:hi, :] = (stage[lo:hi, :] + volb[lo:hi, :] * (scale * o)) * inv
 
+    def arrived(ref, sem):
+        pltpu.make_async_copy(ref, ref, sem).wait()
+
     def x_copy(t, k):
         return pltpu.make_async_remote_copy(
-            src_ref=lmin.at[t], dst_ref=rx.at[k - 1, t],
-            send_sem=sx_s.at[t * 3 + k - 1], recv_sem=sx_r.at[t * 3 + k - 1],
+            src_ref=lmin.at[t], dst_ref=rx.at[t, k - 1], send_sem=sent, recv_sem=x_in.at[t],
             device_id=at_x(k), device_id_type=MESH,
         )
 
     def minimum_of(ts):
+        for t in ts:
+            here = noise.at[t, pl.ds(0, D)]
+            pltpu.make_async_copy(here, here, in_sem.at[7 + t]).wait()
         acc = [jnp.full((K, 128), 3.0e38, F32) for _ in ts]
         for q in range(CHUNKS):
             terms = [[] for _ in ts]
-            for t in ts:
-                noise_in[t][q].wait()
             for d in range(q * per, (q + 1) * per):
                 v = volb[pl.ds(d, K, stride=0), :]
                 for row, t in zip(terms, ts):
@@ -186,71 +191,101 @@
     )
     dinv[...] = 1.0 / ((K * NZ * NY * NC) * vol_d * own_state * (1.0 - own_t))
 
-    sub = lax.broadcasted_iota(jnp.int32, (8, 128), 0)
-    bit2 = (sub & 4) == 0
-    bit1 = (sub & 2) == 0
-    bit0 = (sub & 1) == 0
-
-    def merge(a, b, first, shift):
-        if shift == 4:
-            return jnp.where(first, a, b) + pltpu.roll(jnp.where(first, b, a), 4, axis=0)
-        return jnp.where(
-            first,
-            a + pltpu.roll(a, 8 - shift, axis=0),
-            b + pltpu.roll(b, shift, axis=0),
-        )
-
-    def sums_of(ys):
-        c4 = [merge(ys[s], ys[s + 4], bit2, 4) for s in range(4)]
-        e2 = [merge(c4[s], c4[s + 2], bit1, 2) for s in range(2)]
-        return merge(e2[0], e2[1], bit0, 1)
-
     pl.semaphore_wait(know.at[0], 1)
     pl.semaphore_wait(know.at[1], 1)
     pl.semaphore_wait(know.at[2], 1)
     tell(know.at[3], z_last)
     tell(know.at[4], z_next)
 
+    sub = lax.broadcasted_iota(jnp.int32, (8, 128), 0)
+
+    def swapped(tiles, step):
+        low = (sub & step) == 0
+        out = list(tiles)
+        for a in range(8):
+            if a & step == 0:
+                lo, hi = tiles[a], tiles[a + step]
+                out[a] = jnp.where(low, lo, pltpu.roll(hi, step, axis=0))
+                out[a + step] = jnp.where(low, pltpu.roll(lo, 8 - step, axis=0), hi)
+        return out
+
+    for t in range(4):
+
+        def turn(r, _, t=t):
+            for u in range(4):
+                g = r * 4 + u
+                tiles = [noise[t, g * 8 + s].astype(F32) for s in range(8)]
+                for step in (4, 2, 1):
+                    tiles = swapped(tiles, step)
+                for k in range(8):
+                    turned[t, k, pl.ds(pl.multiple_of(g * 8, 8), 8), :] = tiles[k]
+            return 0
+
+        lax.fori_loop(0, 8, turn, 0)
+
+    pl.semaphore_wait(know.at[3], 1)
+    pl.semaphore_wait(know.at[4], 1)
+    tell(know.at[5], z_last)
+
     def core_copy(t):
         return pltpu.make_async_remote_copy(
-            src_ref=nt.at[t, 1 - c], dst_ref=rc.at[t], send_sem=sc_s.at[t], recv_sem=sc_r.at[t],
+            src_ref=nt.at[t, 1 - c], dst_ref=rc.at[t], send_sem=sent, recv_sem=core_in.at[t],
             device_id=at(z, y, 1 - c), device_id_type=MESH,
         )
+
+    side = {1: 0, 3: 1}
+    y_far = (y + 2) % NY
 
     def y_copy(t, k):
         peer = (y + k) % NY
         return pltpu.make_async_remote_copy(
-            src_ref=nt.at[t, c, peer], dst_ref=ry.at[t, k - 1],
-            send_sem=sy_s.at[t * 3 + k - 1], recv_sem=sy_r.at[t * 3 + k - 1],
+            src_ref=nt.at[t, c, peer], dst_ref=ry.at[t, side[k]],
+            send_sem=sent, recv_sem=y_in.at[t],
             device_id=at(z, peer, c), device_id_type=MESH,
         )
 
+    def far_copy(t, peer, zz):
+        return pltpu.make_async_remote_copy(
+            src_ref=nt.at[t, c, y_far, zz], dst_ref=rf.at[z], send_sem=sent, recv_sem=far_z_in,
+            device_id=at(peer, y, c), device_id_type=MESH,
+        )
+
+    def to_each(t, copy):
+        if t == 3:
+            copy(t, 2 * blocks[t] + 1 - odd, 1 - odd).start()
+        else:
+            for zz in range(2):
+                copy(t, 2 * blocks[t] + zz, zz).start()
+
     def after_core(t):
-        core_copy(t).wait_recv()
+        arrived(rc.at[t], core_in.at[t])
         nt[t, c] = nt[t, c] + rc[t]
-        for k in (2, 1, 3):
+        for k in (1, 3):
             y_copy(t, k).start()
+        if t == 0:
+            pl.semaphore_wait(know.at[5], 1)
+        to_each(t, far_copy)
 
     wsum = [jnp.zeros((8, 128), F32)] * 2
-    small_y = []
     tot[...] = jnp.zeros_like(tot)
     for t, j in enumerate(blocks):
-        for k in (1, 2, 3):
-            x_copy(t, k).wait_recv()
+        arrived(rx.at[t], x_in.at[t])
         least = jnp.minimum(
-            jnp.minimum(lmin[t], rx[0, t]), jnp.minimum(rx[1, t], rx[2, t])
+            jnp.minimum(lmin[t], rx[t, 0]), jnp.minimum(rx[t, 1], rx[t, 2])
         )
         scale = rows_t[1:2, lanes_of(t)]
         payoff = jnp.exp(scale * least)
         p = payoff * scale
         tot[pl.ds(j, 1), :] = jnp.sum(payoff, axis=0, keepdims=True)
+        rows = [jnp.broadcast_to(p[k : k + 1, :], (8, 128)) for k in range(K)]
         for h in range(2):
             tiles = []
             for g in range(16):
                 first = h * 128 + g * 8
-                ys = [noise[t, first + s].astype(F32) * p for s in range(min(8, D - first))]
-                ys += [jnp.zeros((8, 128), F32)] * (8 - len(ys))
-                tiles.append(sums_of(ys))
+                terms = [turned[t, k, first : first + 8, :] * rows[k] for k in range(K)]
+                while len(terms) > 1:
+                    terms = [a + b for a, b in zip(terms[::2], terms[1::2])]
+                tiles.append(terms[0])
             block = jnp.concatenate(tiles, axis=0).T
             part = jnp.zeros((8, 128), F32)
             for q in range(16):
@@ -259,10 +294,6 @@
                 nt[t, cc, yy, zz, :, h * 128 : (h + 1) * 128] = piece
                 part = part + piece
             wsum[h] = wsum[h] + part
-        if t == 0:
-            pl.semaphore_wait(know.at[3], 1)
-            pl.semaphore_wait(know.at[4], 1)
-            tell(know.at[5], z_last)
         if t == 3:
             for h in range(2):
                 tot[4 + h : 5 + h, :] = jnp.sum(wsum[h], axis=0, keepdims=True)
@@ -270,11 +301,10 @@
             smy[me] = tot[...]
             for k in (4, 5, 3, 2, 7, 6, 1):
                 cp = pltpu.make_async_remote_copy(
-                    src_ref=smy.at[me], dst_ref=smy.at[me], send_sem=smy_s.at[k - 1], recv_sem=smy_r.at[k - 1],
+                    src_ref=smy.at[me], dst_ref=smy.at[me], send_sem=sent, recv_sem=small_y_in,
                     device_id=at(z, (y + k // 2) % NY, (c + k) % 2), device_id_type=MESH,
                 )
                 cp.start()
-                small_y.append(cp)
         core_copy(t).start()
 
     for t in range(3):
@@ -283,40 +313,41 @@
 
     def z_copy(t, peer, zz):
         return pltpu.make_async_remote_copy(
-            src_ref=nt.at[t, c, y, zz], dst_ref=rz.at[z], send_sem=sz_s.at[peer], recv_sem=sz_r.at[z],
+            src_ref=nt.at[t, c, y, zz], dst_ref=rz.at[z], send_sem=sent, recv_sem=z_in,
             device_id=at(peer, y, c), device_id_type=MESH,
         )
 
     def after_y(t):
-        for k in range(1, NY):
-            y_copy(t, k).wait_recv()
-        nt[t, c, y] = nt[t, c, y] + (ry[t, 0] + ry[t, 1] + ry[t, 2])
-        base = 2 * blocks[t]
-        if t == 3:
-            z_copy(t, base + 1 - odd, 1 - odd).start()
-        else:
-            for zz in range(2):
-                z_copy(t, base + zz, zz).start()
-
-    pl.semaphore_wait(know.at[5], 1)
-    for cp in small_y:
-        cp.wait_recv()
+        arrived(ry.at[t], y_in.at[t])
+        nt[t, c, y] = nt[t, c, y] + (ry[t, 0] + ry[t, 1])
+        to_each(t, z_copy)
+
+    arrived(smy.at[pl.ds(0, NY * NC - 1)], small_y_in)
     smz[z] = ((smy[0] + smy[1]) + (smy[2] + smy[3])) + ((smy[4] + smy[5]) + (smy[6] + smy[7]))
-    small_z = []
     for k in (4, 3, 5, 2, 6, 1, 7):
         cp = pltpu.make_async_remote_copy(
-            src_ref=smz.at[z], dst_ref=smz.at[z], send_sem=smz_s.at[k - 1], recv_sem=smz_r.at[k - 1],
+            src_ref=smz.at[z], dst_ref=smz.at[z], send_sem=sent, recv_sem=small_z_in,
             device_id=at((z + k) % NZ, y, c), device_id_type=MESH,
         )
         cp.start()
-        small_z.append(cp)
     after_y(0)
     after_y(1)
     after_y(2)
     after_y(3)
-
-    for cp in small_z:
-        cp.wait_recv()
+    others = pl.ds(0, NZ - 1)
+    arrived(rf.at[others], far_z_in)
+    total = nt[3, c, y_far, odd]
+    for k in range(1, NZ):
+        src = (z + k) % NZ
+        total = total + rf[src]
+    far_sum[0] = total
+    far_sent = pltpu.make_async_remote_copy(
+        src_ref=far_sum.at[0], dst_ref=far_sum.at[1], send_sem=sent, recv_sem=far_y_in,
+        device_id=at(z, y_far, c), device_id_type=MESH,
+    )
+    far_sent.start()
+
+    arrived(smz.at[others], small_z_in)
     whole = ((smz[0] + smz[1]) + (smz[2] + smz[3])) + ((smz[4] + smz[5]) + (smz[6] + smz[7]))
     inner = K * NZ * NY * NC
     tot[...] = whole
@@ -342,30 +373,17 @@
     own_row = pltpu.roll(jnp.broadcast_to(own_row, (8, 128)), (128 - (path % 16) * 8) % 128, axis=1)
     pv_ref[...] = own_row[0:1, 0:8]
 
+    arrived(rz.at[others], z_in)
     own = nt[3, c, y, odd]
     for k in range(1, NZ):
         src = (z + k) % NZ
-        pltpu.make_async_remote_copy(
-            src_ref=rz.at[src], dst_ref=rz.at[src], send_sem=sz_s.at[src], recv_sem=sz_r.at[src],
-            device_id=at(src, y, c), device_id_type=MESH,
-        ).wait_recv()
         own = own + rz[src]
+    far_sent.wait_recv()
+    own = own + far_sum[1]
     pg_ref[...] = own[:, 0:D] * dinv[...]
 
-    for cp in small_y + small_z:
-        cp.wait_send()
-    for t in range(4):
-        core_copy(t).wait_send()
-        for k in (1, 2, 3):
-            x_copy(t, k).wait_send()
-        for k in range(1, NY):
-            y_copy(t, k).wait_send()
-    for k in range(1, NZ):
-        peer = (z + k) % NZ
-        pltpu.make_async_remote_copy(
-            src_ref=rz.at[peer], dst_ref=rz.at[peer], send_sem=sz_s.at[peer], recv_sem=sz_r.at[peer],
-            device_id=at(peer, y, c), device_id_type=MESH,
-        ).wait_send()
+    rows_sent = 4 * 3 * 8 + 4 * 128 + 4 * 2 * 32 + 2 * 7 * 16 + 2 * 7 * 8 + 16
+    arrived(bytes_of.at[pl.ds(0, rows_sent)], sent)
 
 
 def hand_out(a, b, c, d, a_out, b_out, c_out, d_out, one, sem):
@@ -390,15 +408,14 @@
         in_specs=[hbm] * 5,
         out_specs=(vmem,) * 4,
         scratch_shapes=[
-            V((4, D, K, 128), BF16), V((D, M), BF16), V((1, D), F32), V((1, D), F32), V((1, M), F32),
+            V((4, 256, K, 128), BF16), V((4, K, 256, 128), F32), V((D, M), BF16), V((1, D), F32), V((1, D), F32), V((1, M), F32),
             V((1, 256), F32), V((1, 256), F32), V((256, 128), F32), V((4, 256, 128), F32),
-            V((4, K, 128), F32), V((3, 4, K, 128), F32), V((8, M), F32), V((256, 128), F32),
+            V((4, K, 128), F32), V((4, 3, K, 128), F32), V((8, M), F32), V((256, 128), F32),
             V((4, NC, NY, 2, 8, 256), F32), V((4, NY, 2, 8, 256), F32),
-            V((4, 3, 2, 8, 256), F32), V((NZ, 8, 256), F32),
+            V((4, 2, 2, 8, 256), F32), V((NZ, 8, 256), F32), V((NZ, 8, 256), F32), V((2, 8, 256), F32), V((1216, 128), F32),
             V((NY * NC, 8, 128), F32), V((NZ, 8, 128), F32), V((8, 128), F32),
             V((8, D), F32),
-            dma((7 + 4 * CHUNKS,)), dma((12,)), dma((12,)), dma((4,)), dma((4,)), dma((12,)), dma((12,)),
-            dma((NZ,)), dma((NZ,)), dma((7,)), dma((7,)), dma((7,)), dma((7,)),
+            dma((11,)), dma, dma((4,)), dma((4,)), dma((4,)), dma, dma, dma, dma, dma,
             pltpu.SemaphoreType.REGULAR((6,)),
         ],
         compiler_params=pltpu.CompilerParams(

time: 24.5 us -> 23.2 us (0.947)
  Pallas kernels: 23.7 us -> 22.4 us
    pallas_call x1, Pallas kernels: 23.1 us -> 21.7 us  [per_device(): pl.pallas_call(kernel, out_shape=(V((1, 128), F32), V((1, D), F32), V((1,...]
where the time goes in v6:
time: 23.2 us; the launch traced here: 23 us
  Pallas kernels  22.4 us (97%)
  between operations  0.64 us (3%)
    pallas_call x1, Pallas kernels, per_device(): pl.pallas_call(kernel, out_shape=(V((1, 128), F32), V((1, D), F32), V((1,...  21.7 us
    pallas_call x1, Pallas kernels, per_device(): pl.pallas_call(hand_out, out_shape=tuple((jax.ShapeDtypeStruct(s, F32) fo...  0.64 us

profile of v6, /device:TPU:1, one launch (start us, length us, event | category | flops | bytes accessed | tf_op | source)
XLA Modules:
  0.0 23.0 jit_solution(8182947388521864456)
XLA Ops:
  0.6 21.7 %shard_map.84 = (f32[1,128]{1,0:T(1,128)S(1)}, f32[1,250]{1,0:T(1,128)S(1)}, f32[1,8]{1,0:T(1,128)S(1)}, f32[8,250]{1,0:T(8,128)S(1)}) custom-call(bf16[250,8,512]{2,1,0:T(8,128)(2,1)} %bitcast.8, bf16[250,512]{1,0:T(8,128)(2,1)} %outer_hbm.1, f32[1,250]{1,0:T(1,128)} %bitcast.10, f32[1,250]{1,0:T(1,128)} %bitcast.11, f32[1,512]{1,0:T(1,128)} %bitcast.9), custom_call_target="tpu_custom_call" | custom-call | tf_op jit(solution)/shard_map/pallas_call | solution.py:405
  22.4 0.6 %shard_map.85 = (f32[1,1]{1,0:T(1,128)}, f32[1,250]{1,0:T(1,128)}, f32[1,8]{1,0:T(1,128)}, f32[8,250]{1,0:T(8,128)}) custom-call(f32[1,128]{1,0:T(1,128)S(1)} %get-tuple-element.12.a, f32[1,250]{1,0:T(1,128)S(1)} %get-tuple-element.13.b, f32[1,8]{1,0:T(1,128)S(1)} %get-tuple-element.14.c, f32[8,250]{1,0:T(8,128)S(1)} %get-tuple-element.15.d), custom_call_target="tpu_custom_call" | custom-call | tf_op jit(solution)/shard_map/pallas_call | solution.py:427

commit v7 on v6

--- a/solution.py
+++ b/solution.py
@@ -70,22 +70,20 @@
         return pl.ds(pl.multiple_of(blocks[t] * 128, 128), 128)
 
     per = D // CHUNKS
-    outer_in = [
-        pltpu.make_async_copy(outer_hbm.at[:, lanes_of(t)], outer.at[:, lanes_of(t)], in_sem.at[3 + t])
-        for t in range(4)
-    ]
     noise_in = [
         [
             pltpu.make_async_copy(
                 noise_hbm.at[pl.ds(q * per, per), :, lanes_of(t)],
                 noise.at[t, pl.ds(q * per, per)],
-                in_sem.at[7 + t],
+                in_sem.at[4 + t],
             )
             for q in range(CHUNKS)
         ]
         for t in range(4)
     ]
-    for cp in [outer_in[0]] + noise_in[0]:
+    outer_in = pltpu.make_async_copy(outer_hbm, outer, in_sem.at[3])
+    outer_in.start()
+    for cp in noise_in[0]:
         cp.start()
 
     barrier = pltpu.get_barrier_semaphore()
@@ -101,7 +99,7 @@
     z_next, z_last = at((z + 1) % NZ, y, c), at((z + NZ - 1) % NZ, y, c)
 
     for t in range(1, 4):
-        for cp in [outer_in[t]] + noise_in[t]:
+        for cp in noise_in[t]:
             cp.start()
     for t in range(4):
         noise[t, D:] = jnp.zeros((256 - D, K, 128), BF16)
@@ -132,7 +130,6 @@
     rows_t[2:3, :] = inv_root_tau
 
     def coefficients(t):
-        outer_in[t].wait()
         scale = rows_t[0:1, lanes_of(t)]
         inv = rows_t[2:3, lanes_of(t)]
         for lo in range(0, D, 16):
@@ -152,7 +149,7 @@
     def minimum_of(ts):
         for t in ts:
             here = noise.at[t, pl.ds(0, D)]
-            pltpu.make_async_copy(here, here, in_sem.at[7 + t]).wait()
+            pltpu.make_async_copy(here, here, in_sem.at[4 + t]).wait()
         acc = [jnp.full((K, 128), 3.0e38, F32) for _ in ts]
         for q in range(CHUNKS):
             terms = [[] for _ in ts]
@@ -164,9 +161,10 @@
         for t, a in zip(ts, acc):
             lmin[t] = a
 
+    outer_in.wait()
+    for t in range(4):
+        coefficients(t)
     for ts in ((0,), (1,), (2, 3)):
-        for t in ts:
-            coefficients(t)
         minimum_of(ts)
         if ts[0] == 0:
             pl.semaphore_wait(barrier, len(near))
@@ -223,10 +221,6 @@
 
         lax.fori_loop(0, 8, turn, 0)
 
-    pl.semaphore_wait(know.at[3], 1)
-    pl.semaphore_wait(know.at[4], 1)
-    tell(know.at[5], z_last)
-
     def core_copy(t):
         return pltpu.make_async_remote_copy(
             src_ref=nt.at[t, 1 - c], dst_ref=rc.at[t], send_sem=sent, recv_sem=core_in.at[t],
@@ -260,11 +254,11 @@
     def after_core(t):
         arrived(rc.at[t], core_in.at[t])
         nt[t, c] = nt[t, c] + rc[t]
-        for k in (1, 3):
-            y_copy(t, k).start()
         if t == 0:
             pl.semaphore_wait(know.at[5], 1)
         to_each(t, far_copy)
+        for k in (1, 3):
+            y_copy(t, k).start()
 
     wsum = [jnp.zeros((8, 128), F32)] * 2
     tot[...] = jnp.zeros_like(tot)
@@ -306,6 +300,10 @@
                 )
                 cp.start()
         core_copy(t).start()
+        if t == 1:
+            pl.semaphore_wait(know.at[3], 1)
+            pl.semaphore_wait(know.at[4], 1)
+            tell(know.at[5], z_last)
 
     for t in range(3):
         after_core(t)
@@ -415,7 +413,7 @@
             V((4, 2, 2, 8, 256), F32), V((NZ, 8, 256), F32), V((NZ, 8, 256), F32), V((2, 8, 256), F32), V((1216, 128), F32),
             V((NY * NC, 8, 128), F32), V((NZ, 8, 128), F32), V((8, 128), F32),
             V((8, D), F32),
-            dma((11,)), dma, dma((4,)), dma((4,)), dma((4,)), dma, dma, dma, dma, dma,
+            dma((8,)), dma, dma((4,)), dma((4,)), dma((4,)), dma, dma, dma, dma, dma,
             pltpu.SemaphoreType.REGULAR((6,)),
         ],
         compiler_params=pltpu.CompilerParams(

time: 23.2 us -> 22.8 us (0.983)
  Pallas kernels: 22.4 us -> 22.1 us
    pallas_call x1, Pallas kernels: 21.7 us -> 21.4 us  [per_device(): pl.pallas_call(kernel, out_shape=(V((1, 128), F32), V((1, D), F32), V((1,...]
where the time goes in v7:
time: 22.8 us; the launch traced here: 22.7 us
  Pallas kernels  22.1 us (97%)
  between operations  0.64 us (3%)
    pallas_call x1, Pallas kernels, per_device(): pl.pallas_call(kernel, out_shape=(V((1, 128), F32), V((1, D), F32), V((1,...  21.4 us
    pallas_call x1, Pallas kernels, per_device(): pl.pallas_call(hand_out, out_shape=tuple((jax.ShapeDtypeStruct(s, F32) fo...  0.64 us

profile of v7, /device:TPU:1, one launch (start us, length us, event | category | flops | bytes accessed | tf_op | source)
XLA Modules:
  0.0 22.7 jit_solution(5678910594187789627)
XLA Ops:
  0.6 21.4 %shard_map.84 = (f32[1,128]{1,0:T(1,128)S(1)}, f32[1,250]{1,0:T(1,128)S(1)}, f32[1,8]{1,0:T(1,128)S(1)}, f32[8,250]{1,0:T(8,128)S(1)}) custom-call(bf16[250,8,512]{2,1,0:T(8,128)(2,1)} %bitcast.8, bf16[250,512]{1,0:T(8,128)(2,1)} %outer_hbm.1, f32[1,250]{1,0:T(1,128)} %bitcast.10, f32[1,250]{1,0:T(1,128)} %bitcast.11, f32[1,512]{1,0:T(1,128)} %bitcast.9), custom_call_target="tpu_custom_call" | custom-call | tf_op jit(solution)/shard_map/pallas_call | solution.py:403
  22.1 0.6 %shard_map.85 = (f32[1,1]{1,0:T(1,128)}, f32[1,250]{1,0:T(1,128)}, f32[1,8]{1,0:T(1,128)}, f32[8,250]{1,0:T(8,128)}) custom-call(f32[1,128]{1,0:T(1,128)S(1)} %get-tuple-element.12.a, f32[1,250]{1,0:T(1,128)S(1)} %get-tuple-element.13.b, f32[1,8]{1,0:T(1,128)S(1)} %get-tuple-element.14.c, f32[8,250]{1,0:T(8,128)S(1)} %get-tuple-element.15.d), custom_call_target="tpu_custom_call" | custom-call | tf_op jit(solution)/shard_map/pallas_call | solution.py:425

commit v8 on v7

--- a/solution.py
+++ b/solution.py
@@ -407,7 +407,7 @@
         out_specs=(vmem,) * 4,
         scratch_shapes=[
             V((4, 256, K, 128), BF16), V((4, K, 256, 128), F32), V((D, M), BF16), V((1, D), F32), V((1, D), F32), V((1, M), F32),
-            V((1, 256), F32), V((1, 256), F32), V((256, 128), F32), V((4, 256, 128), F32),
+            V((1, 256), F32), V((1, 256), F32), V((264, 128), F32), V((4, 264, 128), F32),
             V((4, K, 128), F32), V((4, 3, K, 128), F32), V((8, M), F32), V((256, 128), F32),
             V((4, NC, NY, 2, 8, 256), F32), V((4, NY, 2, 8, 256), F32),
             V((4, 2, 2, 8, 256), F32), V((NZ, 8, 256), F32), V((NZ, 8, 256), F32), V((2, 8, 256), F32), V((1216, 128), F32),

time: 22.8 us -> 22.9 us (level)
  no operation moved by 1% of the time
where the time goes in v8:
time: 22.9 us; the launch traced here: 22.7 us
  Pallas kernels  22.1 us (97%)
  between operations  0.64 us (3%)
    pallas_call x1, Pallas kernels, per_device(): pl.pallas_call(kernel, out_shape=(V((1, 128), F32), V((1, D), F32), V((1,...  21.5 us
    pallas_call x1, Pallas kernels, per_device(): pl.pallas_call(hand_out, out_shape=tuple((jax.ShapeDtypeStruct(s, F32) fo...  0.64 us

profile of v8, /device:TPU:1, one launch (start us, length us, event | category | flops | bytes accessed | tf_op | source)
XLA Modules:
  0.0 22.7 jit_solution(8706957471442711955)
XLA Ops:
  0.6 21.5 %shard_map.84 = (f32[1,128]{1,0:T(1,128)S(1)}, f32[1,250]{1,0:T(1,128)S(1)}, f32[1,8]{1,0:T(1,128)S(1)}, f32[8,250]{1,0:T(8,128)S(1)}) custom-call(bf16[250,8,512]{2,1,0:T(8,128)(2,1)} %bitcast.8, bf16[250,512]{1,0:T(8,128)(2,1)} %outer_hbm.1, f32[1,250]{1,0:T(1,128)} %bitcast.10, f32[1,250]{1,0:T(1,128)} %bitcast.11, f32[1,512]{1,0:T(1,128)} %bitcast.9), custom_call_target="tpu_custom_call" | custom-call | tf_op jit(solution)/shard_map/pallas_call | solution.py:403
  22.1 0.6 %shard_map.85 = (f32[1,1]{1,0:T(1,128)}, f32[1,250]{1,0:T(1,128)}, f32[1,8]{1,0:T(1,128)}, f32[8,250]{1,0:T(8,128)}) custom-call(f32[1,128]{1,0:T(1,128)S(1)} %get-tuple-element.12.a, f32[1,250]{1,0:T(1,128)S(1)} %get-tuple-element.13.b, f32[1,8]{1,0:T(1,128)S(1)} %get-tuple-element.14.c, f32[8,250]{1,0:T(8,128)S(1)} %get-tuple-element.15.d), custom_call_target="tpu_custom_call" | custom-call | tf_op jit(solution)/shard_map/pallas_call | solution.py:425

commit v9 on v7

--- a/solution.py
+++ b/solution.py
@@ -75,7 +75,7 @@
             pltpu.make_async_copy(
                 noise_hbm.at[pl.ds(q * per, per), :, lanes_of(t)],
                 noise.at[t, pl.ds(q * per, per)],
-                in_sem.at[4 + t],
+                in_sem.at[4 + min(t, 2)],
             )
             for q in range(CHUNKS)
         ]
@@ -142,14 +142,13 @@
 
     def x_copy(t, k):
         return pltpu.make_async_remote_copy(
-            src_ref=lmin.at[t], dst_ref=rx.at[t, k - 1], send_sem=sent, recv_sem=x_in.at[t],
+            src_ref=lmin.at[t], dst_ref=rx.at[t, k - 1], send_sem=sent, recv_sem=x_in.at[min(t, 2)],
             device_id=at_x(k), device_id_type=MESH,
         )
 
     def minimum_of(ts):
-        for t in ts:
-            here = noise.at[t, pl.ds(0, D)]
-            pltpu.make_async_copy(here, here, in_sem.at[4 + t]).wait()
+        here = noise.at[pl.ds(ts[0], len(ts)), pl.ds(0, D)]
+        pltpu.make_async_copy(here, here, in_sem.at[4 + ts[0]]).wait()
         acc = [jnp.full((K, 128), 3.0e38, F32) for _ in ts]
         for q in range(CHUNKS):
             terms = [[] for _ in ts]
@@ -263,7 +262,10 @@
     wsum = [jnp.zeros((8, 128), F32)] * 2
     tot[...] = jnp.zeros_like(tot)
     for t, j in enumerate(blocks):
-        arrived(rx.at[t], x_in.at[t])
+        if t < 2:
+            arrived(rx.at[t], x_in.at[t])
+        elif t == 2:
+            arrived(rx.at[pl.ds(2, 2)], x_in.at[2])
         least = jnp.minimum(
             jnp.minimum(lmin[t], rx[t, 0]), jnp.minimum(rx[t, 1], rx[t, 2])
         )
@@ -413,7 +415,7 @@
             V((4, 2, 2, 8, 256), F32), V((NZ, 8, 256), F32), V((NZ, 8, 256), F32), V((2, 8, 256), F32), V((1216, 128), F32),
             V((NY * NC, 8, 128), F32), V((NZ, 8, 128), F32), V((8, 128), F32),
             V((8, D), F32),
-            dma((8,)), dma, dma((4,)), dma((4,)), dma((4,)), dma, dma, dma, dma, dma,
+            dma((7,)), dma, dma((3,)), dma((4,)), dma((4,)), dma, dma, dma, dma, dma,
             pltpu.SemaphoreType.REGULAR((6,)),
         ],
         compiler_params=pltpu.CompilerParams(

time: 22.8 us -> 23.1 us (1.013)
  no operation moved by 1% of the time
where the time goes in v9:
time: 23.1 us; the launch traced here: 22.9 us
  Pallas kernels  22.3 us (97%)
  between operations  0.64 us (3%)
    pallas_call x1, Pallas kernels, per_device(): pl.pallas_call(kernel, out_shape=(V((1, 128), F32), V((1, D), F32), V((1,...  21.7 us
    pallas_call x1, Pallas kernels, per_device(): pl.pallas_call(hand_out, out_shape=tuple((jax.ShapeDtypeStruct(s, F32) fo...  0.64 us

profile of v9, /device:TPU:1, one launch (start us, length us, event | category | flops | bytes accessed | tf_op | source)
XLA Modules:
  0.0 22.9 jit_solution(13125299401405266506)
XLA Ops:
  0.6 21.7 %shard_map.84 = (f32[1,128]{1,0:T(1,128)S(1)}, f32[1,250]{1,0:T(1,128)S(1)}, f32[1,8]{1,0:T(1,128)S(1)}, f32[8,250]{1,0:T(8,128)S(1)}) custom-call(bf16[250,8,512]{2,1,0:T(8,128)(2,1)} %bitcast.8, bf16[250,512]{1,0:T(8,128)(2,1)} %outer_hbm.1, f32[1,250]{1,0:T(1,128)} %bitcast.10, f32[1,250]{1,0:T(1,128)} %bitcast.11, f32[1,512]{1,0:T(1,128)} %bitcast.9), custom_call_target="tpu_custom_call" | custom-call | tf_op jit(solution)/shard_map/pallas_call | solution.py:405
  22.3 0.6 %shard_map.85 = (f32[1,1]{1,0:T(1,128)}, f32[1,250]{1,0:T(1,128)}, f32[1,8]{1,0:T(1,128)}, f32[8,250]{1,0:T(8,128)}) custom-call(f32[1,128]{1,0:T(1,128)S(1)} %get-tuple-element.12.a, f32[1,250]{1,0:T(1,128)S(1)} %get-tuple-element.13.b, f32[1,8]{1,0:T(1,128)S(1)} %get-tuple-element.14.c, f32[8,250]{1,0:T(8,128)S(1)} %get-tuple-element.15.d), custom_call_target="tpu_custom_call" | custom-call | tf_op jit(solution)/shard_map/pallas_call | solution.py:427
